TPU v7x, 32 devices: a whole 2x2x4 slice. The times are simulated.
32 devices in a mesh: freq: 8 (over z, x), tm: 4 (over y, core).
Axes of the slice: x: 2, y: 2, z: 4, core: 2. Of those that a mesh axis runs over, the one named last changes fastest.
Arguments:
- vis: float32 [2, 32, 16, 1891], P(None, 'freq', 'tm'), may hold values from -12 to 12
- coherency: float32 [10, 2, 32, 16, 1891], P(None, None, 'freq', 'tm'), may hold values from -3 to 3
- pairs: int32 [2, 1891], replicated, may hold values from 0 to 61, as said below
- rho: float32 [10], replicated, may hold values from 30 to 300
- gains: float32 [2, 32, 10, 62], P(None, 'freq'), may hold values from -5 to 5
- duals: float32 [2, 32, 10, 62], P(None, 'freq'), may hold values from -50 to 50
- consensus: float32 [2, 4, 10, 62], replicated, may hold values from -5 to 5
Outputs:
- solved: float32 [2, 32, 10, 62], P(None, 'freq')
- duals_new: float32 [2, 32, 10, 62], P(None, 'freq')
- consensus_new: float32 [2, 4, 10, 62], replicated
Inputs may be any that keep to these rules, and one draw needn't show every extreme that they name: `pairs`: every unordered pair of two different stations of 0 to 61 is one baseline, exactly once, in an arbitrary order and orientation.
All inputs are finite; a program needn't handle non-finite values.
Results may differ from a plain program's by a relative error of at most 0.0003.
Values sent between devices are 32-bit elements; how exact they have to be, the bound alone decides.
No kernel may reach another device: no remote copies, remote signals or barrier semaphores. Data moves between devices by JAX's collectives and lax.ppermute only.
A program may use at most 64 MiB of HBM per device.

v0:
```python
import jax
import jax.numpy as jnp
from jax import lax
from jax.sharding import PartitionSpec as P

SWEEPS = 4


highest = lax.Precision.HIGHEST


def basis_rows(start, count, total):
    position = (start + jnp.arange(count, dtype=jnp.int32)).astype(jnp.float32)
    upper = (position + 0.5) / total
    lower = 1.0 - upper
    return jnp.stack(
        [
            lower * lower * lower,
            3.0 * upper * lower * lower,
            3.0 * upper * upper * lower,
            upper * upper * upper,
        ]
    )


def one_hot(station, count):
    return (station[:, None] == jnp.arange(count, dtype=jnp.int32)[None, :]).astype(jnp.float32)


def normal_terms(vis, coherency, gains, first, second):
    gain_first = jnp.einsum("rcks,bs->rkcb", gains, first, precision=highest)[:, :, :, None, :]
    gain_second = jnp.einsum("rcks,bs->rkcb", gains, second, precision=highest)[:, :, :, None, :]
    coh_real = coherency[:, 0]
    coh_imag = coherency[:, 1]
    lead_real = coh_real * gain_second[0] + coh_imag * gain_second[1]
    lead_imag = coh_imag * gain_second[0] - coh_real * gain_second[1]
    model_real = gain_first[0] * lead_real - gain_first[1] * lead_imag
    model_imag = gain_first[0] * lead_imag + gain_first[1] * lead_real
    error_real = vis[0] - jnp.sum(model_real, axis=0)
    error_imag = vis[1] - jnp.sum(model_imag, axis=0)
    resid_real = error_real[None] + model_real
    resid_imag = error_imag[None] + model_imag
    tail_real = coh_real * gain_first[0] - coh_imag * gain_first[1]
    tail_imag = coh_real * gain_first[1] + coh_imag * gain_first[0]
    first_real = jnp.sum(resid_real * lead_real + resid_imag * lead_imag, axis=2)
    first_imag = jnp.sum(resid_imag * lead_real - resid_real * lead_imag, axis=2)
    second_real = jnp.sum(resid_real * tail_real + resid_imag * tail_imag, axis=2)
    second_imag = jnp.sum(resid_real * tail_imag - resid_imag * tail_real, axis=2)
    first_power = jnp.sum(lead_real * lead_real + lead_imag * lead_imag, axis=2)
    second_power = jnp.sum(tail_real * tail_real + tail_imag * tail_imag, axis=2)

    def stations(by_first, by_second):
        return jnp.einsum("kcb,bs->cks", by_first, first, precision=highest) + jnp.einsum(
            "kcb,bs->cks", by_second, second, precision=highest
        )

    return (
        stations(first_real, second_real),
        stations(first_imag, second_imag),
        stations(first_power, second_power),
    )


def refine(gains, numer_real, numer_imag, power, target, rho):
    scale = power + rho[None, :, None]
    fresh = jnp.stack([(numer_real + target[0]) / scale, (numer_imag + target[1]) / scale])
    return 0.5 * (gains + fresh)


def fit_consensus(rhs, basis):
    gram = jnp.dot(basis, basis.T, precision=highest)
    factor = jnp.linalg.cholesky(gram)
    flat = jnp.moveaxis(rhs, 1, 0).reshape(rhs.shape[1], -1)
    solved = jax.scipy.linalg.cho_solve((factor, True), flat)
    return jnp.moveaxis(
        solved.reshape(rhs.shape[1], rhs.shape[0], rhs.shape[2], rhs.shape[3]), 0, 1
    )


def local(vis, coherency, pairs, rho, gains, duals, consensus):
    per_device = gains.shape[1]
    station_count = gains.shape[3]
    total = per_device * lax.axis_size("freq")
    offset = lax.axis_index("freq") * per_device
    local_basis = basis_rows(offset, per_device, total)
    first = one_hot(pairs[0], station_count)
    second = one_hot(pairs[1], station_count)
    prior = jnp.einsum("mc,rmks->rcks", local_basis, consensus, precision=highest)
    target = rho[None, None, :, None] * prior - duals
    for sweep in range(SWEEPS):
        numer_real, numer_imag, power = normal_terms(vis, coherency, gains, first, second)
        numer_real, numer_imag, power = lax.psum((numer_real, numer_imag, power), "tm")
        gains = refine(gains, numer_real, numer_imag, power, target, rho)
    weighted = gains + duals / rho[None, None, :, None]
    piece = lax.all_gather(weighted, "freq", axis=1, tiled=True)
    rows = basis_rows(jnp.int32(0), piece.shape[1], total)
    rhs = jnp.einsum("mc,rcks->rmks", rows, piece, precision=highest)
    consensus_new = fit_consensus(rhs, basis_rows(0, total, total))
    prior_new = jnp.einsum("mc,rmks->rcks", local_basis, consensus_new, precision=highest)
    duals_new = duals + rho[None, None, :, None] * (gains - prior_new)
    return (gains, duals_new, consensus_new)


def solution(mesh):
    in_specs = (
        P(None, "freq", "tm", None),
        P(None, None, "freq", "tm", None),
        P(),
        P(),
        P(None, "freq", None, None),
        P(None, "freq", None, None),
        P(),
    )
    out_specs = (P(None, "freq", None, None), P(None, "freq", None, None), P())
    return jax.shard_map(local, mesh=mesh, in_specs=in_specs, out_specs=out_specs, check_vma=False)
```

profile of v0, /device:TPU:0, one launch (start us, length us, event | category | flops | bytes accessed | tf_op | source)
XLA Modules:
  0.0 142.8 jit_solution(8561696226693263801)
XLA Ops:
  0.6 0.8 slice_reduce_fusion.1
  1.5 1.3 convolution_bitcast_fusion.7
  2.9 0.1 copy.74
  3.0 0.1 copy.79
  3.2 0.5 copy-done.3
  3.7 0.5 convolution_bitcast_fusion.6
  4.3 0.1 copy.77
  4.4 0.1 copy.78
  4.6 1.4 copy-done.1
  5.9 2.0 %fusion.170 = (f32[4,4,1891]{2,1,0:T(4,128)S(1)}, f32[4,4,1891]{2,1,0:T(4,128)S(1)}, f32[10,4,4,1891]{3,2,1,0:T(4,128)S(1)}, f32[10,4,4,1891]{3,2,1,0:T(4,128)S(...) fusion(f32[10,4,1891]{2,1,0:T(4,128)S(1)} %copy.79, f32[10,4,1891]{2,1,0:T(4,128)S(1)} %copy.74, ...), kind=kLoop, calls=%fused_computation.284 | loop fusion | flops 5990688 | bytes 8713728 | tf_op jit(solution)/shard_map/reduce_sum | solution.py:39
  8.0 6.7 %add_reduce_fusion.14 = (f32[10,4,1891]{2,1,0:T(4,128)S(1)}, f32[10,4,1891]{2,1,0:T(4,128)S(1)}, f32[10,4,1891]{2,1,0:T(4,128)S(1)}, f32[10,4,1891]{2,1,0:T(4,12...) fusion(f32[10,4,4,1891]{3,2,1,0:T(4,128)S(1)} %get-tuple-element.75, ...), kind=kLoop, calls=%fused_computation.84 | loop fusion | flops 9228080 | bytes 7503488 | tf_op jit(solution)/shard_map/reduce_sum | solution.py:47
  14.8 0.4 fusion.62
  15.2 0.4 fusion.27
  15.7 0.4 fusion.59
  16.1 0.4 fusion.26
  16.5 0.4 fusion.56
  16.9 0.4 fusion.25
  17.4 14.0 %all-reduce.3 = (f32[4,10,62]{2,1,0:T(8,128)S(1)}, f32[4,10,62]{2,1,0:T(8,128)S(1)}, f32[4,10,62]{2,1,0:T(8,128)S(1)}) all-reduce(f32[4,10,62]{2,1,0:T(8,128)S(1)} %fusion.25, f32[4,10,62]{2,1,0:T(8,128)S(1)} %fusion.26, f32[4,10,62]{2,1,0:T(8,128)S(1)} %fusion.27), channel_id=1, replica_groups=mesh['freq'=8,'tm'=4] {'tm'}, use_global_device_ids=true, to_apply=%region_10.0 | all-reduce | flops 7440 | bytes 59520 | tf_op jit(solution)/shard_map/psum | solution.py:92
  31.5 0.2 fusion.187
  31.9 0.5 convolution_bitcast_fusion.4
  32.8 0.5 convolution_bitcast_fusion.5
  33.7 2.0 %fusion.172 = (f32[4,4,1891]{2,1,0:T(4,128)S(1)}, f32[4,4,1891]{2,1,0:T(4,128)S(1)}, f32[10,4,4,1891]{3,2,1,0:T(4,128)S(1)}, f32[10,4,4,1891]{3,2,1,0:T(4,128)S(...) fusion(f32[10,4,1891]{2,1,0:T(4,128)S(1)} %copy.92, f32[10,4,1891]{2,1,0:T(4,128)S(1)} %copy.89, ...), kind=kLoop, calls=%fused_computation.286 | loop fusion | flops 5990688 | bytes 8713728 | tf_op jit(solution)/shard_map/reduce_sum | solution.py:39
  35.8 6.7 %add_reduce_fusion.10 = (f32[10,4,1891]{2,1,0:T(4,128)S(1)}, f32[10,4,1891]{2,1,0:T(4,128)S(1)}, f32[10,4,1891]{2,1,0:T(4,128)S(1)}, f32[10,4,1891]{2,1,0:T(4,12...) fusion(f32[10,4,4,1891]{3,2,1,0:T(4,128)S(1)} %get-tuple-element.73, ...), kind=kLoop, calls=%fused_computation.76 | loop fusion | flops 9228080 | bytes 7503488 | tf_op jit(solution)/shard_map/reduce_sum | solution.py:47
  42.5 0.4 fusion.53
  43.0 0.4 fusion.24
  43.4 0.4 fusion.50
  43.8 0.4 fusion.23
  44.2 0.4 fusion.47
  44.7 0.4 fusion.22
  45.1 11.4 %all-reduce.2 = (f32[4,10,62]{2,1,0:T(8,128)S(1)}, f32[4,10,62]{2,1,0:T(8,128)S(1)}, f32[4,10,62]{2,1,0:T(8,128)S(1)}) all-reduce(f32[4,10,62]{2,1,0:T(8,128)S(1)} %fusion.22, f32[4,10,62]{2,1,0:T(8,128)S(1)} %fusion.23, f32[4,10,62]{2,1,0:T(8,128)S(1)} %fusion.24), channel_id=1, replica_groups=mesh['freq'=8,'tm'=4] {'tm'}, use_global_device_ids=true, to_apply=%region_21.0 | all-reduce | flops 7440 | bytes 59520 | tf_op jit(solution)/shard_map/psum | solution.py:92
  56.6 0.5 convolution_bitcast_fusion.2
  57.4 0.5 convolution_bitcast_fusion.3
  58.3 2.0 %fusion.174 = (f32[4,4,1891]{2,1,0:T(4,128)S(1)}, f32[4,4,1891]{2,1,0:T(4,128)S(1)}, f32[10,4,4,1891]{3,2,1,0:T(4,128)S(1)}, f32[10,4,4,1891]{3,2,1,0:T(4,128)S(...) fusion(f32[10,4,1891]{2,1,0:T(4,128)S(1)} %copy.102, f32[10,4,1891]{2,1,0:T(4,128)S(1)} %copy.99, ...), kind=kLoop, calls=%fused_computation.288 | loop fusion | flops 5990688 | bytes 8713728 | tf_op jit(solution)/shard_map/reduce_sum | solution.py:39
  60.5 6.7 %add_reduce_fusion.6 = (f32[10,4,1891]{2,1,0:T(4,128)S(1)}, f32[10,4,1891]{2,1,0:T(4,128)S(1)}, f32[10,4,1891]{2,1,0:T(4,128)S(1)}, f32[10,4,1891]{2,1,0:T(4,128...) fusion(f32[10,4,4,1891]{3,2,1,0:T(4,128)S(1)} %get-tuple-element.71, ...), kind=kLoop, calls=%fused_computation.68 | loop fusion | flops 9228080 | bytes 7503488 | tf_op jit(solution)/shard_map/reduce_sum | solution.py:47
  67.2 0.4 fusion.44
  67.6 0.4 fusion.21
  68.1 0.4 fusion.41
  68.5 0.4 fusion.20
  68.9 0.4 fusion.38
  69.3 0.4 fusion.19
  69.8 11.4 %all-reduce.1 = (f32[4,10,62]{2,1,0:T(8,128)S(1)}, f32[4,10,62]{2,1,0:T(8,128)S(1)}, f32[4,10,62]{2,1,0:T(8,128)S(1)}) all-reduce(f32[4,10,62]{2,1,0:T(8,128)S(1)} %fusion.19, f32[4,10,62]{2,1,0:T(8,128)S(1)} %fusion.20, f32[4,10,62]{2,1,0:T(8,128)S(1)} %fusion.21), channel_id=1, replica_groups=mesh['freq'=8,'tm'=4] {'tm'}, use_global_device_ids=true, to_apply=%region_32.0 | all-reduce | flops 7440 | bytes 59520 | tf_op jit(solution)/shard_map/psum | solution.py:92
  81.2 0.5 convolution_bitcast_fusion
  82.1 0.5 convolution_bitcast_fusion.1
  83.0 2.0 %fusion.176 = (f32[4,4,1891]{2,1,0:T(4,128)S(1)}, f32[4,4,1891]{2,1,0:T(4,128)S(1)}, f32[10,4,4,1891]{3,2,1,0:T(4,128)S(1)}, f32[10,4,4,1891]{3,2,1,0:T(4,128)S(...) fusion(f32[10,4,1891]{2,1,0:T(4,128)S(1)} %copy.112, f32[10,4,1891]{2,1,0:T(4,128)S(1)} %copy.109, ...), kind=kLoop, calls=%fused_computation.290 | loop fusion | flops 5990688 | bytes 8713728 | tf_op jit(solution)/shard_map/reduce_sum | solution.py:39
  85.1 6.7 %add_reduce_fusion.2 = (f32[10,4,1891]{2,1,0:T(4,128)S(1)}, f32[10,4,1891]{2,1,0:T(4,128)S(1)}, f32[10,4,1891]{2,1,0:T(4,128)S(1)}, f32[10,4,1891]{2,1,0:T(4,128...) fusion(f32[10,4,4,1891]{3,2,1,0:T(4,128)S(1)} %get-tuple-element.69, ...), kind=kLoop, calls=%fused_computation.60 | loop fusion | flops 9228080 | bytes 7503488 | tf_op jit(solution)/shard_map/reduce_sum | solution.py:47
  91.9 0.4 fusion.35
  92.3 0.4 fusion.18
  92.7 0.4 fusion.32
  93.2 0.4 fusion.17
  93.6 0.4 fusion.29
  94.0 0.4 fusion.16
  94.4 11.6 %all-reduce = (f32[4,10,62]{2,1,0:T(8,128)S(1)}, f32[4,10,62]{2,1,0:T(8,128)S(1)}, f32[4,10,62]{2,1,0:T(8,128)S(1)}) all-reduce(f32[4,10,62]{2,1,0:T(8,128)S(1)} %fusion.16, f32[4,10,62]{2,1,0:T(8,128)S(1)} %fusion.17, f32[4,10,62]{2,1,0:T(8,128)S(1)} %fusion.18), channel_id=1, replica_groups=mesh['freq'=8,'tm'=4] {'tm'}, use_global_device_ids=true, to_apply=%region_43.0 | all-reduce | flops 7440 | bytes 59520 | tf_op jit(solution)/shard_map/psum | solution.py:92
  106.2 31.6 %all_gather.3 = f32[2,32,10,62]{3,2,1,0:T(8,128)S(1)} all-gather(f32[2,4,10,62]{3,2,1,0:T(8,128)S(1)} %get-tuple-element.58), channel_id=1, replica_groups=mesh['freq'=8,'tm'=4] {'freq'}, dimensions={1}, use_global_device_ids=true | all-gather | bytes 178560 | tf_op jit(solution)/shard_map/all_gather | solution.py:95
  137.8 0.4 fusion.100
  138.4 0.1 fusion.162
  138.7 0.4 cholesky.16
  139.1 0.6 compare_reduce_fusion
  139.7 0.6 fusion.152
  140.4 0.3 custom-call.10
  140.7 0.3 fusion.150
  141.0 0.2 convolution_bitcast_fusion.8
  141.2 0.2 fusion.188
  141.5 0.6 copy.129
  142.2 0.6 copy.128
  (55 shorter events, 3.4 us)
Async XLA Ops:
  0.6 30.9 %copy-start = (f32[2,4,10,62]{3,1,2,0:T(4,128)S(1)}, f32[2,4,10,62]{3,1,2,0:T(4,128)}, u32[]{:S(2)}) copy-start(f32[2,4,10,62]{3,1,2,0:T(4,128)} %param.13) | copy-start | bytes 59524
  2.9 0.8 copy-start.3
  4.2 1.7 %copy-start.1 = (f32[10,2,4,4,1891]{4,3,2,1,0:T(4,128)S(1)}, f32[10,2,4,4,1891]{4,3,2,1,0:T(4,128)}, u32[]{:S(2)}) copy-start(f32[10,2,4,4,1891]{4,3,2,1,0:T(4,128)} %param.8) | copy-start | bytes 7261444
  5.9 2.0 %copy-start.2 = (f32[2,4,4,1891]{3,2,1,0:T(4,128)S(1)}, f32[2,4,4,1891]{3,2,1,0:T(4,128)}, u32[]{:S(2)}) copy-start(f32[2,4,4,1891]{3,2,1,0:T(4,128)} %param.7) | copy-start | bytes 726148
  15.6 16.1 %copy-start.4 = (f32[2,4,10,62]{3,1,2,0:T(4,128)S(1)}, f32[2,4,10,62]{3,1,2,0:T(4,128)}, u32[]{:S(2)}) copy-start(f32[2,4,10,62]{3,1,2,0:T(4,128)} %param.12) | copy-start | bytes 59524
  15.6 16.1 %copy-start.6 = (f32[10]{0:T(128)S(1)}, f32[10]{0:T(128)}, u32[]{:S(2)}) copy-start(f32[10]{0:T(128)} %param.10) | copy-start | bytes 124
  141.2 1.6 %copy-start.5 = (f32[2,4,10,62]{3,1,2,0:T(4,128)}, f32[2,4,10,62]{3,1,2,0:T(4,128)S(1)}, u32[]{:S(2)}) copy-start(f32[2,4,10,62]{3,1,2,0:T(4,128)S(1)} %convolution_bitcast_fusion.8) | copy-start | bytes 59524
where the time goes:
time: 143 us
  blocking collectives  80 us (56%)
  other arithmetic  38.1 us (27%)
  matrix products  16.7 us (12%)
  local copies, waits for them, and re-layouts  6.78 us (5%)
    psum x4, blocking collectives, local(): lax.psum((numer_real, numer_imag, power), 'tm')  48.4 us
    all_gather x1, blocking collectives, local(): piece = lax.all_gather(weighted, 'freq', axis=1, tiled=True)  31.6 us
    reduce_sum x4, other arithmetic, normal_terms(): jnp.sum(resid_real * tail_real + resid_imag * tail_imag, axis=2)  26.9 us
    reduce_sum x4, other arithmetic, normal_terms(): error_real = vis[0] - jnp.sum(model_real, axis=0)  8.16 us
    dot_general x12, matrix products, stations(): jnp.einsum('kcb,bs->cks', by_second, second, precision=highest)  5.07 us
    dot_general x12, matrix products, stations(): jnp.einsum('kcb,bs->cks', by_first, first, precision=highest)  5.06 us
    unnamed x16, local copies, waits for them, and re-layouts  3.18 us
    dot_general x4, matrix products, normal_terms(): jnp.einsum('rcks,bs->rkcb', gains, first, precision=highest)  2.96 us

commit v1 on v0

v1 whole, which is shorter than its diff:
```python
import functools

import jax
import jax.numpy as jnp
import numpy as np
from jax import lax
from jax.experimental import pallas as pl
from jax.experimental.pallas import tpu as pltpu
from jax.sharding import PartitionSpec as P

SWEEPS = 4
LANES = 128
HALF = 64

highest = lax.Precision.HIGHEST


def basis_values(upper):
    lower = 1.0 - upper
    return (
        lower * lower * lower,
        3.0 * upper * lower * lower,
        3.0 * upper * upper * lower,
        upper * upper * upper,
    )


def gram_inverse(total):
    rows = np.stack(basis_values((np.arange(total) + 0.5) / total))
    return np.linalg.inv(rows @ rows.T)


def pick(index, values):
    out = values[-1]
    for m in range(len(values) - 2, -1, -1):
        out = jnp.where(index == m, values[m], out)
    return out


def evaluate(offset, rows, per, total, terms):
    row = lax.broadcasted_iota(jnp.int32, (rows, rows // per * terms), 0)
    col = lax.broadcasted_iota(jnp.int32, (rows, rows // per * terms), 1)
    upper = ((offset + row % per).astype(jnp.float32) + 0.5) / total
    value = pick(col % terms, basis_values(upper))
    return jnp.where(row // per == col // terms, value, 0.0)


def project(offset, rows, per, total, terms):
    row = lax.broadcasted_iota(jnp.int32, (rows // per * terms, rows), 0)
    col = lax.broadcasted_iota(jnp.int32, (rows // per * terms, rows), 1)
    upper = ((offset + col % per).astype(jnp.float32) + 0.5) / total
    values = basis_values(upper)
    inverse = gram_inverse(total)
    mixed = [
        functools.reduce(jnp.add, [float(inverse[m, n]) * values[n] for n in range(terms)])
        for m in range(terms)
    ]
    return jnp.where(row // terms == col // per, pick(row % terms, mixed), 0.0)


def rho_rows(rho_ref, rows, per):
    index = lax.broadcasted_iota(jnp.int32, (rows, LANES), 0) // per
    out = jnp.full((rows, LANES), rho_ref[0], jnp.float32)
    for k in range(1, rows // per):
        out = jnp.where(index == k, rho_ref[k], out)
    return out


def pack(native_ref, packed_ref, count):
    _, directions, per, _ = native_ref.shape
    packed_ref[...] = jnp.zeros(packed_ref.shape, jnp.float32)
    for k in range(directions):
        for r in range(2):
            packed_ref[k * per:(k + 1) * per, r * HALF:r * HALF + count] = native_ref[r, k]


def unpack(packed, scratch_ref, native_ref):
    _, directions, per, count = native_ref.shape
    scratch_ref[...] = packed
    for k in range(directions):
        for r in range(2):
            native_ref[r, k] = scratch_ref[k * per:(k + 1) * per, r * HALF:r * HALF + count]


def total_of(parts):
    while len(parts) > 1:
        parts = [parts[i] + parts[i + 1] for i in range(0, len(parts), 2)]
    return parts[0]


def split_rows(rows):
    return -(-(rows // 2) // 8) * 8


def refine(sums, gains, target, rho):
    rows = gains.shape[0]
    top = split_rows(rows)
    numer = sums[:rows]
    tail = sums[rows:]
    power = jnp.concatenate([tail[:, :HALF], tail[:rows - top, HALF:]], axis=0)
    power = jnp.concatenate([power, power], axis=1)
    return 0.5 * (gains + (numer + target) / (power + rho))


def gather_rows(gains):
    rows = jnp.concatenate([gains[:, :HALF], gains[:, HALF:]], axis=0)
    high = rows.astype(jnp.bfloat16).astype(jnp.float32)
    return jnp.concatenate([high, rows - high], axis=1).astype(jnp.bfloat16)


def hot(pairs_row):
    index = lax.broadcasted_iota(jnp.int32, (LANES, pairs_row.shape[1]), 0) % HALF
    return jnp.where(index == pairs_row, 1.0, 0.0).astype(jnp.bfloat16)


def places(rows, times):
    power = 2 * times * rows
    seen = power + rows
    height = max(seen + 2 * times * 8, times * rows + 8 * rows, seen + times * 8 + 64)
    return power, seen, -(-height // 8) * 8


def sweep_tile(j, per, times, tile_ref, at_ref, by_first, by_second):
    rows = at_ref.shape[1] // 4
    pow_at, vis_at, _ = places(rows, times)
    groups = rows // 8

    def gained(i):
        return at_ref[j, i * rows:(i + 1) * rows, :].reshape(groups, 8, LANES)

    p_real, p_imag, q_real, q_imag = [gained(i) for i in range(4)]
    m_real = p_real * q_real + p_imag * q_imag
    m_imag = p_imag * q_real - p_real * q_imag
    weight = tile_ref[j, pow_at:pow_at + rows, :].reshape(groups, 8, LANES)
    s_real = m_real * weight
    s_imag = m_imag * weight

    def over_directions(x):
        x = jnp.sum(x, axis=0)
        shift = per
        while shift < 8:
            x = x + pltpu.roll(x, shift, 0)
            shift *= 2
        return x

    for t in range(times):
        c_real = tile_ref[j, t * rows:(t + 1) * rows, :].reshape(groups, 8, LANES)
        c_imag = tile_ref[j, (times + t) * rows:(times + t + 1) * rows, :].reshape(groups, 8, LANES)
        e_real = tile_ref[j, vis_at + t * 8:vis_at + t * 8 + 8, :] - over_directions(m_real * c_real - m_imag * c_imag)
        e_imag = tile_ref[j, vis_at + (times + t) * 8:vis_at + (times + t) * 8 + 8, :] - over_directions(m_real * c_imag + m_imag * c_real)
        s_real = s_real + (e_real * c_real + e_imag * c_imag)
        s_imag = s_imag + (e_imag * c_real - e_real * c_imag)

    def put(ref, real, imag, power):
        stack = jnp.concatenate([x.reshape(rows, LANES) for x in (real, imag, power)], axis=0)
        high = stack.astype(jnp.bfloat16).astype(jnp.float32)
        ref[j] = jnp.concatenate([high, stack - high], axis=0).astype(jnp.bfloat16)

    put(
        by_first,
        s_real * q_real - s_imag * q_imag,
        s_real * q_imag + s_imag * q_real,
        weight * (q_real * q_real + q_imag * q_imag),
    )
    put(
        by_second,
        s_real * p_real + s_imag * p_imag,
        s_real * p_imag - s_imag * p_real,
        weight * (p_real * p_real + p_imag * p_imag),
    )


def sweep_block(gains, pairs_ref, tiles, per, times, tile_ref, at_ref, by_first, by_second):
    rows = gains.shape[0]
    left = gather_rows(gains)
    pairs = pairs_ref[...]
    first = hot(pairs[0:1])
    second = hot(pairs[1:2])
    for side, choice in enumerate((first, second)):
        at_all = jnp.dot(left, choice, preferred_element_type=jnp.float32)
        for j in range(tiles):
            at_ref[j, side * 2 * rows:(side + 1) * 2 * rows, :] = at_all[:, j * LANES:(j + 1) * LANES]

    def step(j, carry):
        sweep_tile(j, per, times, tile_ref, at_ref, by_first, by_second)
        return carry

    lax.fori_loop(0, tiles, step, 0)
    across = (((1,), (1,)), ((), ()))
    sums = 0.0
    for ref, choice in ((by_first, first), (by_second, second)):
        laid = jnp.concatenate([ref[j] for j in range(tiles)], axis=1)
        sums = sums + lax.dot_general(laid, choice[:HALF], across, preferred_element_type=jnp.float32)
    return sums[:3 * rows] + sums[3 * rows:]


def join(sums, rows):
    top = split_rows(rows)
    power = sums[2 * rows:]
    low = jnp.concatenate([power[top:], jnp.zeros((2 * top - rows, HALF), jnp.float32)], axis=0)
    return jnp.concatenate(
        [
            jnp.concatenate([sums[:rows], sums[rows:2 * rows]], axis=1),
            jnp.concatenate([power[:top], low], axis=1),
        ],
        axis=0,
    )


def opening_kernel(
    sizes, offset_ref, rho_ref, coh_in, vis_in, pairs_ref, gains_in, duals_in, cons_in,
    tile_ref, gains_ref, target_ref, sums_ref,
    acc_ref, pad_ref, at_ref, by_first, by_second,
):
    per, times, total, count, pairs_count, tiles = sizes
    directions = coh_in.shape[0]
    rows = directions * per
    pow_at, vis_at, _ = places(rows, times)
    step = pl.program_id(0)

    @pl.when(step == 0)
    def _():
        pack(gains_in, gains_ref, count)
        pack(cons_in, pad_ref, count)
        terms = cons_in.shape[2]
        prior = jnp.dot(
            evaluate(offset_ref[0], rows, per, total, terms), pad_ref[...],
            precision=highest, preferred_element_type=jnp.float32,
        )
        pack(duals_in, target_ref, count)
        target_ref[...] = rho_rows(rho_ref, rows, per) * prior - target_ref[...]
        acc_ref[...] = jnp.zeros(acc_ref.shape, jnp.float32)

    for j in range(tiles):
        lanes = slice(j * LANES, (j + 1) * LANES)
        place = (step * tiles + j) * LANES + lax.broadcasted_iota(jnp.int32, (times, LANES), 1)
        keep = place < pairs_count
        for r in range(2):
            for c in range(per):
                block = jnp.where(keep, vis_in[r, c, :, lanes], 0.0)
                for copy in range(8 // per):
                    tile_ref[j, pl.ds(vis_at + r * times * 8 + copy * per + c, times, stride=8), :] = block
                for k in range(directions):
                    tile_ref[j, pl.ds(r * times * rows + k * per + c, times, stride=rows), :] = jnp.where(
                        keep, coh_in[k, r, c, :, lanes], 0.0
                    )
        power = jnp.zeros((rows, LANES), jnp.float32)
        for t in range(2 * times):
            c_part = tile_ref[j, t * rows:(t + 1) * rows, :]
            power = power + c_part * c_part
        tile_ref[j, pow_at:pow_at + rows, :] = power

    acc_ref[...] += sweep_block(
        gains_ref[...], pairs_ref, tiles, per, times, tile_ref, at_ref, by_first, by_second
    )

    @pl.when(step == pl.num_programs(0) - 1)
    def _():
        sums_ref[...] = join(acc_ref[...], rows)


def sweep_kernel(sizes, ways, rho_ref, *refs):
    per, times, total, count, pairs_count, tiles = sizes
    parts = refs[:ways]
    gains_in, target_ref, tile_ref, pairs_ref, gains_ref, sums_ref = refs[ways:ways + 6]
    at_ref, by_first, by_second = refs[ways + 6:]
    rows = gains_in.shape[0]
    gains = refine(
        total_of([part[...] for part in parts]), gains_in[...], target_ref[...], rho_rows(rho_ref, rows, per)
    )
    gains_ref[...] = gains
    sums_ref[...] = join(
        sweep_block(
            gains, pairs_ref, tile_ref.shape[0], per, times, tile_ref, at_ref, by_first, by_second
        ),
        rows,
    )


def closing_kernel(sizes, terms, ways, offset_ref, rho_ref, *refs):
    per, times, total, count, pairs_count, tiles = sizes
    parts = refs[:ways]
    gains_in, target_ref, duals_in, gains_ref, solved_ref, fit_ref, pad_ref = refs[ways:]
    rows = gains_in.shape[0]
    rho = rho_rows(rho_ref, rows, per)
    gains = refine(total_of([part[...] for part in parts]), gains_in[...], target_ref[...], rho)
    pack(duals_in, pad_ref, count)
    weighted = gains + pad_ref[...] / rho
    fit_ref[...] = jnp.dot(
        project(offset_ref[0], rows, per, total, terms), weighted,
        precision=highest, preferred_element_type=jnp.float32,
    )
    gains_ref[...] = gains
    unpack(gains, pad_ref, solved_ref)


def final_kernel(sizes, ways, offset_ref, rho_ref, *refs):
    per, times, total, count, pairs_count, tiles = sizes
    parts = refs[:ways]
    gains_ref, duals_in, duals_ref, cons_ref, pad_ref, cons_pad = refs[ways:]
    rows = gains_ref.shape[0]
    terms = cons_ref.shape[2]
    cons = total_of([part[...] for part in parts])
    prior = jnp.dot(
        evaluate(offset_ref[0], rows, per, total, terms), cons,
        precision=highest, preferred_element_type=jnp.float32,
    )
    pack(duals_in, pad_ref, count)
    fresh = pad_ref[...] + rho_rows(rho_ref, rows, per) * (gains_ref[...] - prior)
    unpack(fresh, pad_ref, duals_ref)
    unpack(cons, cons_pad, cons_ref)


def exchange(x, axis, strides):
    count = lax.axis_size(axis)
    return [x] + [lax.ppermute(x, axis, [(i, i ^ s) for i in range(count)]) for s in strides]


def shape_of(*dims, dtype=jnp.float32):
    return jax.ShapeDtypeStruct(dims, dtype)


vmem = pl.BlockSpec(memory_space=pltpu.VMEM)
smem = pl.BlockSpec(memory_space=pltpu.SMEM)


def local(vis, coherency, pairs, rho, gains, duals, consensus):
    directions, _, per, times, pairs_count = coherency.shape
    count = gains.shape[3]
    terms = consensus.shape[1]
    rows = directions * per
    total = per * lax.axis_size("freq")
    offset = (lax.axis_index("freq") * per).astype(jnp.int32).reshape(1)
    all_tiles = -(-pairs_count // LANES)
    tiles = max(d for d in range(1, 6) if all_tiles % d == 0)
    steps = all_tiles // tiles
    width = tiles * LANES
    pairs = jnp.pad(pairs, ((0, 8 - pairs.shape[0]), (0, all_tiles * LANES - pairs_count)), constant_values=-1)
    gains = jnp.swapaxes(gains, 1, 2)
    duals = jnp.swapaxes(duals, 1, 2)
    consensus = jnp.swapaxes(consensus, 1, 2)
    sizes = (per, times, total, count, pairs_count, tiles)
    sum_rows = rows + split_rows(rows)
    height = places(rows, times)[2]
    packed = shape_of(rows, LANES)

    def work(blocks):
        return [
            pltpu.VMEM((blocks, 4 * rows, LANES), jnp.float32),
            pltpu.VMEM((blocks, 6 * rows, LANES), jnp.bfloat16),
            pltpu.VMEM((blocks, 6 * rows, LANES), jnp.bfloat16),
        ]

    tile_data, gains_now, target, sums = pl.pallas_call(
        functools.partial(opening_kernel, sizes),
        name="opening",
        grid=(steps,),
        in_specs=[
            smem,
            smem,
            pl.BlockSpec((directions, 2, per, times, width), lambda i: (0, 0, 0, 0, i)),
            pl.BlockSpec((2, per, times, width), lambda i: (0, 0, 0, i)),
            pl.BlockSpec((8, width), lambda i: (0, i)),
            pl.BlockSpec(gains.shape, lambda i: (0, 0, 0, 0)),
            pl.BlockSpec(duals.shape, lambda i: (0, 0, 0, 0)),
            pl.BlockSpec(consensus.shape, lambda i: (0, 0, 0, 0)),
        ],
        out_specs=[
            pl.BlockSpec((tiles, height, LANES), lambda i: (i, 0, 0)),
            pl.BlockSpec((rows, LANES), lambda i: (0, 0)),
            pl.BlockSpec((rows, LANES), lambda i: (0, 0)),
            pl.BlockSpec((sum_rows, LANES), lambda i: (0, 0)),
        ],
        out_shape=[
            shape_of(all_tiles, height, LANES),
            packed,
            packed,
            shape_of(sum_rows, LANES),
        ],
        scratch_shapes=[
            pltpu.VMEM((3 * rows, HALF), jnp.float32),
            pltpu.VMEM((rows, LANES), jnp.float32),
        ] + work(tiles),
    )(offset, rho, coherency, vis, pairs, gains, duals, consensus)

    ways = lax.axis_size("tm")
    peers = range(1, ways)
    for _ in range(SWEEPS - 1):
        gains_now, sums = pl.pallas_call(
            functools.partial(sweep_kernel, sizes, ways),
            name="sweep",
            in_specs=[smem] + [vmem] * (ways + 4),
            out_specs=[vmem, vmem],
            out_shape=[packed, shape_of(sum_rows, LANES)],
            scratch_shapes=work(all_tiles),
        )(rho, *exchange(sums, "tm", peers), gains_now, target, tile_data, pairs)

    gains_now, solved, fit = pl.pallas_call(
        functools.partial(closing_kernel, sizes, terms, ways),
        name="closing",
        in_specs=[smem, smem] + [vmem] * (ways + 3),
        out_specs=[vmem] * 3,
        out_shape=[packed, shape_of(2, directions, per, count), shape_of(directions * terms, LANES)],
        scratch_shapes=[pltpu.VMEM((rows, LANES), jnp.float32)],
    )(offset, rho, *exchange(sums, "tm", peers), gains_now, target, duals)

    span = lax.axis_size("freq")
    stride = 1
    while stride * 4 < span:
        fit = total_of(exchange(fit, "freq", [stride, 2 * stride, 3 * stride]))
        stride *= 4
    parts = exchange(fit, "freq", range(stride, span, stride))
    duals_new, consensus_new = pl.pallas_call(
        functools.partial(final_kernel, sizes, len(parts)),
        name="final",
        in_specs=[smem, smem] + [vmem] * (len(parts) + 2),
        out_specs=[vmem] * 2,
        out_shape=[shape_of(2, directions, per, count), shape_of(2, directions, terms, count)],
        scratch_shapes=[
            pltpu.VMEM((rows, LANES), jnp.float32),
            pltpu.VMEM((directions * terms, LANES), jnp.float32),
        ],
    )(offset, rho, *parts, gains_now, duals)
    return tuple(jnp.swapaxes(x, 1, 2) for x in (solved, duals_new, consensus_new))


def solution(mesh):
    in_specs = (
        P(None, "freq", "tm", None),
        P(None, None, "freq", "tm", None),
        P(),
        P(),
        P(None, "freq", None, None),
        P(None, "freq", None, None),
        P(),
    )
    out_specs = (P(None, "freq", None, None), P(None, "freq", None, None), P())
    return jax.shard_map(local, mesh=mesh, in_specs=in_specs, out_specs=out_specs, check_vma=False)
```

time: 143 us -> 64.8 us (0.45)
  blocking collectives: 80 us -> 0 us
  other arithmetic: 38.1 us -> 0.73 us
  Pallas kernels: 0 us -> 26.3 us
  waiting for transfers between devices: 0 us -> 17.3 us
  matrix products: 16.7 us -> 0 us
  starting transfers between devices: 0 us -> 14.9 us
  local copies, waits for them, and re-layouts: 6.78 us -> 4.42 us
    psum x4 -> x0, blocking collectives: 48.4 us -> none  [local(): lax.psum((numer_real, numer_imag, power), 'tm')]
    reduce_sum x8 -> x0, other arithmetic: 35.1 us -> none  [the longest x4 26.9 us: normal_terms(): jnp.sum(resid_real * tail_real + resid_imag * tail_imag, axis=2)]
    all_gather x1 -> x0, blocking collectives: 31.6 us -> none  [local(): piece = lax.all_gather(weighted, 'freq', axis=1, tiled=True)]
    pallas_call x0 -> x6, Pallas kernels: none -> 26.3 us  [the longest x3 16 us: local(): pl.pallas_call(functools.partial(sweep_kernel, sizes, ways), name='sweep'...]
    ppermute x0 -> x16, waiting for transfers between devices: none -> 17.3 us  [exchange(): lax.ppermute(x, axis, [(i, i ^ s) for i in range(count)])]
    dot_general x36 -> x0, matrix products: 16.2 us -> none  [the longest x12 5.07 us: stations(): jnp.einsum('kcb,bs->cks', by_second, second, precision=highest)]
    ppermute x0 -> x16, starting transfers between devices: none -> 14.9 us  [exchange(): lax.ppermute(x, axis, [(i, i ^ s) for i in range(count)])]
    mul x24 -> x0, local copies, waits for them, and re-layouts: 2.46 us -> none  [the longest x12 1.23 us: normal_terms(): lead_real = coh_real * gain_second[0] + coh_imag * gain_second[1]]
  transfers between devices with their start and end apart: 0 -> 16, of which waited for: 0 -> 12; matrix products, arithmetic and copies ran while one was open for 0% -> 0% of each run, Pallas kernels for 0% -> 0%
where the time goes in v1:
time: 64.8 us; the launch traced here: 64.4 us
  Pallas kernels  26.3 us (41%)
  waiting for transfers between devices  17.3 us (27%)
  starting transfers between devices  14.9 us (23%)
  local copies, waits for them, and re-layouts  4.42 us (7%)
  other arithmetic  0.73 us (1%)
  between operations  0.69 us (1%)
    ppermute x16, waiting for transfers between devices, exchange(): lax.ppermute(x, axis, [(i, i ^ s) for i in range(count)])  17.3 us
    pallas_call x3, Pallas kernels, local(): pl.pallas_call(functools.partial(sweep_kernel, sizes, ways), name='sweep'...  16 us
    ppermute x16, starting transfers between devices, exchange(): lax.ppermute(x, axis, [(i, i ^ s) for i in range(count)])  14.9 us
    pallas_call x1, Pallas kernels, local(): pl.pallas_call(functools.partial(opening_kernel, sizes), name='opening',...  6.8 us
    unnamed x28, local copies, waits for them, and re-layouts  3.07 us
    pallas_call x1, Pallas kernels, local(): pl.pallas_call(functools.partial(closing_kernel, sizes, terms, ways), nam...  1.81 us
    pallas_call x1, Pallas kernels, local(): pl.pallas_call(functools.partial(final_kernel, sizes, len(parts)), name='...  1.73 us
    pad x1, local copies, waits for them, and re-layouts, local(): jnp.pad(pairs, ((0, 8 - pairs.shape[0]), (0, all_tiles * LANES - pairs_co...  1.35 us
  transfers between devices with their start and end apart: 16, of which 12 were waited for; matrix products, arithmetic and copies ran while one was open for 0% of the time, Pallas kernels for 0%

profile of v1, /device:TPU:0, one launch (start us, length us, event | category | flops | bytes accessed | tf_op | source)
XLA Modules:
  0.0 64.4 jit_solution(10463220823163791905)
XLA Ops:
  0.6 1.3 %pad.4.pairs_ref.refs_7_ = s32[8,1920]{1,0:T(8,128)} pad(s32[2,1891]{1,0:T(2,128)} %param.9, s32[]{:T(128)} %constant.9.clone.1), padding=0_6x0_29 | pad | bytes 76572 | tf_op jit(solution)/shard_map/jit(_pad)/pad | solution.py:338
  2.0 6.8 %opening.1 = (f32[15,480,128]{2,1,0:T(8,128)}, f32[40,128]{1,0:T(8,128)}, f32[40,128]{1,0:T(8,128)}, f32[64,128]{1,0:T(8,128)}) custom-call(s32[1]{0:T(128)} %bitcast.offset_ref, f32[10]{0:T(128)} %rho_ref.11, f32[10,2,4,4,1891]{4,3,2,1,0:T(4,128)} %coh_in.1, f32[2,4,4,1891]{3,2,1,0:T(4,128)} %vis_in.1, s32[8,1920]{1,0:T(8,128)} %pad.4.pairs_ref.refs_7_, ...), custom_call_target="tpu_custom_call" | custom-call | tf_op jit(solution)/shard_map/opening/pallas_call | solution.py:354
  8.8 2.5 %collective-permute-start.2 = (f32[64,128]{1,0:T(8,128)}, f32[64,128]{1,0:T(8,128)S(1)}, u32[]{:S(2)}, u32[]{:S(2)}) collective-permute-start(f32[64,128]{1,0:T(8,128)} %get-tuple-element.18.refs_0_), channel_id=1, source_target_pairs={{0,3},{1,2},{2,1},{3,0},{4,7},{5,6},{6,5},{7,4},{8,11},{9,10},{10,... | collective-permute-start | bytes 98312 | tf_op jit(solution)/shard_map/ppermute | solution.py:316
  11.3 0.6 collective-permute-start.1
  11.9 0.0 collective-permute-start
  12.0 1.4 %collective-permute-done.2.refs_3_ = f32[64,128]{1,0:T(8,128)S(1)} collective-permute-done((f32[64,128]{1,0:T(8,128)}, f32[64,128]{1,0:T(8,128)S(1)}, u32[]{:S(2)}, u32[]{:S(2)}) %collective-permute-start.2) | collective-permute-done | bytes 32800 | tf_op jit(solution)/shard_map/ppermute | solution.py:316
  13.4 0.0 copy-start.2
  13.4 2.1 %collective-permute-done.1.refs_2_ = f32[64,128]{1,0:T(8,128)S(1)} collective-permute-done((f32[64,128]{1,0:T(8,128)}, f32[64,128]{1,0:T(8,128)S(1)}, u32[]{:S(2)}, u32[]{:S(2)}) %collective-permute-start.1) | collective-permute-done | bytes 32800 | tf_op jit(solution)/shard_map/ppermute | solution.py:316
  15.5 0.0 copy-start.5
  15.5 0.0 collective-permute-done.refs_1_
  15.5 0.0 copy-start.8
  15.5 0.0 copy-done.2
  15.5 0.6 copy-done.5
  16.1 0.0 copy-done.8
  16.1 5.3 %sweep.3 = (f32[40,128]{1,0:T(8,128)}, f32[64,128]{1,0:T(8,128)}) custom-call(f32[10]{0:T(128)} %rho_ref.11, f32[64,128]{1,0:T(8,128)} %get-tuple-element.18.refs_0_, f32[64,128]{1,0:T(8,128)} %copy-done.8, f32[64,128]{1,0:T(8,128)} %copy-done.5, f32[64,128]{1,0:T(8,128)} %copy-done.2, f32[40,128]{1,0:T(8,128)} %get-tuple-element.19.refs_4_, ...), custom_call_target="tpu_custom_call" | custom-call | tf_op jit(solution)/shard_map/sweep/pallas_call | solution.py:389
  21.4 0.7 %collective-permute-start.5 = (f32[64,128]{1,0:T(8,128)}, f32[64,128]{1,0:T(8,128)S(1)}, u32[]{:S(2)}, u32[]{:S(2)}) collective-permute-start(f32[64,128]{1,0:T(8,128)} %get-tuple-element.22.refs_0_), channel_id=1, source_target_pairs={{0,3},{1,2},{2,1},{3,0},{4,7},{5,6},{6,5},{7,4},{8,11},{9,10},{10,... | collective-permute-start | bytes 98312 | tf_op jit(solution)/shard_map/ppermute | solution.py:316
  22.1 0.8 %collective-permute-start.4 = (f32[64,128]{1,0:T(8,128)}, f32[64,128]{1,0:T(8,128)S(1)}, u32[]{:S(2)}, u32[]{:S(2)}) collective-permute-start(f32[64,128]{1,0:T(8,128)} %get-tuple-element.22.refs_0_), channel_id=1, source_target_pairs={{0,2},{1,3},{2,0},{3,1},{4,6},{5,7},{6,4},{7,5},{8,10},{9,11},{10,... | collective-permute-start | bytes 98312 | tf_op jit(solution)/shard_map/ppermute | solution.py:316
  22.9 0.4 collective-permute-start.3
  23.3 2.0 %collective-permute-done.5.refs_3_ = f32[64,128]{1,0:T(8,128)S(1)} collective-permute-done((f32[64,128]{1,0:T(8,128)}, f32[64,128]{1,0:T(8,128)S(1)}, u32[]{:S(2)}, u32[]{:S(2)}) %collective-permute-start.5) | collective-permute-done | bytes 32800 | tf_op jit(solution)/shard_map/ppermute | solution.py:316
  25.3 0.0 copy-start.3
  25.3 0.9 %collective-permute-done.4.refs_2_ = f32[64,128]{1,0:T(8,128)S(1)} collective-permute-done((f32[64,128]{1,0:T(8,128)}, f32[64,128]{1,0:T(8,128)S(1)}, u32[]{:S(2)}, u32[]{:S(2)}) %collective-permute-start.4) | collective-permute-done | bytes 32800 | tf_op jit(solution)/shard_map/ppermute | solution.py:316
  26.2 0.0 copy-start.6
  26.2 0.0 collective-permute-done.3.refs_1_
  26.2 0.0 copy-start.9
  26.2 0.0 copy-done.3
  26.2 0.6 copy-done.6
  26.8 0.0 copy-done.9
  26.9 5.3 %sweep.4 = (f32[40,128]{1,0:T(8,128)}, f32[64,128]{1,0:T(8,128)}) custom-call(f32[10]{0:T(128)} %rho_ref.11, f32[64,128]{1,0:T(8,128)} %get-tuple-element.22.refs_0_, f32[64,128]{1,0:T(8,128)} %copy-done.9, f32[64,128]{1,0:T(8,128)} %copy-done.6, f32[64,128]{1,0:T(8,128)} %copy-done.3, f32[40,128]{1,0:T(8,128)} %get-tuple-element.23.refs_4_, ...), custom_call_target="tpu_custom_call" | custom-call | tf_op jit(solution)/shard_map/sweep/pallas_call | solution.py:389
  32.2 0.3 collective-permute-start.8
  32.5 0.6 collective-permute-start.7
  33.1 1.0 %collective-permute-start.6 = (f32[64,128]{1,0:T(8,128)}, f32[64,128]{1,0:T(8,128)S(1)}, u32[]{:S(2)}, u32[]{:S(2)}) collective-permute-start(f32[64,128]{1,0:T(8,128)} %get-tuple-element.24.refs_0_), channel_id=1, source_target_pairs={{0,1},{1,0},{2,3},{3,2},{4,5},{5,4},{6,7},{7,6},{8,9},{9,8},{10,11... | collective-permute-start | bytes 98312 | tf_op jit(solution)/shard_map/ppermute | solution.py:316
  34.0 1.7 %collective-permute-done.8.refs_3_ = f32[64,128]{1,0:T(8,128)S(1)} collective-permute-done((f32[64,128]{1,0:T(8,128)}, f32[64,128]{1,0:T(8,128)S(1)}, u32[]{:S(2)}, u32[]{:S(2)}) %collective-permute-start.8) | collective-permute-done | bytes 32800 | tf_op jit(solution)/shard_map/ppermute | solution.py:316
  35.7 0.0 copy-start.1
  35.7 0.9 %collective-permute-done.7.refs_2_ = f32[64,128]{1,0:T(8,128)S(1)} collective-permute-done((f32[64,128]{1,0:T(8,128)}, f32[64,128]{1,0:T(8,128)S(1)}, u32[]{:S(2)}, u32[]{:S(2)}) %collective-permute-start.7) | collective-permute-done | bytes 32800 | tf_op jit(solution)/shard_map/ppermute | solution.py:316
  36.6 0.0 copy-start.4
  36.6 0.0 collective-permute-done.6.refs_1_
  36.6 0.0 copy-start.7
  36.7 0.0 copy-done.1
  36.7 0.6 copy-done.4
  37.3 0.0 copy-done.7
  37.3 5.3 %sweep.5 = (f32[40,128]{1,0:T(8,128)}, f32[64,128]{1,0:T(8,128)}) custom-call(f32[10]{0:T(128)} %rho_ref.11, f32[64,128]{1,0:T(8,128)} %get-tuple-element.24.refs_0_, f32[64,128]{1,0:T(8,128)} %copy-done.7, f32[64,128]{1,0:T(8,128)} %copy-done.4, f32[64,128]{1,0:T(8,128)} %copy-done.1, f32[40,128]{1,0:T(8,128)} %get-tuple-element.25.refs_4_, ...), custom_call_target="tpu_custom_call" | custom-call | tf_op jit(solution)/shard_map/sweep/pallas_call | solution.py:389
  42.6 0.5 collective-permute-start.11
  43.1 1.0 %collective-permute-start.10 = (f32[64,128]{1,0:T(8,128)}, f32[64,128]{1,0:T(8,128)S(1)}, u32[]{:S(2)}, u32[]{:S(2)}) collective-permute-start(f32[64,128]{1,0:T(8,128)} %get-tuple-element.26.refs_0_), channel_id=1, source_target_pairs={{0,2},{1,3},{2,0},{3,1},{4,6},{5,7},{6,4},{7,5},{8,10},{9,11},{10,... | collective-permute-start | bytes 98312 | tf_op jit(solution)/shard_map/ppermute | solution.py:316
  44.0 0.4 collective-permute-start.9
  44.5 2.0 %collective-permute-done.11.refs_3_ = f32[64,128]{1,0:T(8,128)S(1)} collective-permute-done((f32[64,128]{1,0:T(8,128)}, f32[64,128]{1,0:T(8,128)S(1)}, u32[]{:S(2)}, u32[]{:S(2)}) %collective-permute-start.11) | collective-permute-done | bytes 32800 | tf_op jit(solution)/shard_map/ppermute | solution.py:316
  46.5 0.0 copy-start.10
  46.5 0.7 %collective-permute-done.10.refs_2_ = f32[64,128]{1,0:T(8,128)S(1)} collective-permute-done((f32[64,128]{1,0:T(8,128)}, f32[64,128]{1,0:T(8,128)S(1)}, u32[]{:S(2)}, u32[]{:S(2)}) %collective-permute-start.10) | collective-permute-done | bytes 32800 | tf_op jit(solution)/shard_map/ppermute | solution.py:316
  47.2 0.0 collective-permute-done.9.refs_1_
  47.2 0.0 copy-done.10
  47.2 0.6 copy-done.11
  47.8 0.0 copy-done.12
  47.8 1.8 %closing.1 = (f32[40,128]{1,0:T(8,128)}, f32[2,10,4,62]{3,2,1,0:T(4,128)}, f32[40,128]{1,0:T(8,128)}) custom-call(s32[1]{0:T(128)} %bitcast.offset_ref, f32[10]{0:T(128)} %rho_ref.11, f32[64,128]{1,0:T(8,128)} %get-tuple-element.26.refs_0_, f32[64,128]{1,0:T(8,128)} %copy-done.12, f32[64,128]{1,0:T(8,128)} %copy-done.11, f32[64,128]{1,0:T(8,128)} %copy-done.10, ...), custom_call_target="tpu_custom_call" | custom-call | tf_op jit(solution)/shard_map/closing/pallas_call | solution.py:398
  49.6 2.5 %collective-permute-start.14 = (f32[40,128]{1,0:T(8,128)}, f32[40,128]{1,0:T(8,128)S(1)}, u32[]{:S(2)}, u32[]{:S(2)}) collective-permute-start(f32[40,128]{1,0:T(8,128)} %get-tuple-element.29), channel_id=1, source_target_pairs={{0,12},{4,8},{8,4},{12,0},{16,28},{20,24},{24,20},{28,16},{1,13},{... | collective-permute-start | bytes 61448 | tf_op jit(solution)/shard_map/ppermute | solution.py:316
  52.1 0.4 collective-permute-start.13
  52.6 0.5 collective-permute-start.12
  53.1 1.5 %collective-permute-done.14 = f32[40,128]{1,0:T(8,128)S(1)} collective-permute-done((f32[40,128]{1,0:T(8,128)}, f32[40,128]{1,0:T(8,128)S(1)}, u32[]{:S(2)}, u32[]{:S(2)}) %collective-permute-start.14) | collective-permute-done | bytes 20512 | tf_op jit(solution)/shard_map/ppermute | solution.py:316
  54.6 1.5 %collective-permute-done.13 = f32[40,128]{1,0:T(8,128)S(1)} collective-permute-done((f32[40,128]{1,0:T(8,128)}, f32[40,128]{1,0:T(8,128)S(1)}, u32[]{:S(2)}, u32[]{:S(2)}) %collective-permute-start.13) | collective-permute-done | bytes 20512 | tf_op jit(solution)/shard_map/ppermute | solution.py:316
  56.1 0.4 collective-permute-done.12
  56.6 0.7 %add_add_fusion.refs_0_ = f32[40,128]{1,0:T(8,128)S(1)} fusion(f32[40,128]{1,0:T(8,128)S(1)} %collective-permute-done.13, f32[40,128]{1,0:T(8,128)S(1)} %collective-permute-done.14, f32[40,128]{1,0:T(8,128)} %get-tuple-element.29, f32[40,128]{1,0:T(8,128)S(1)} %collective-permute-done.12), kind=kLoop, calls=%fused_computation | loop fusion | flops 15360 | bytes 102400 | tf_op jit(solution)/shard_map/add | solution.py:87
  57.3 2.7 %collective-permute-start.15 = (f32[40,128]{1,0:T(8,128)S(1)}, f32[40,128]{1,0:T(8,128)S(1)}, u32[]{:S(2)}, u32[]{:S(2)}) collective-permute-start(f32[40,128]{1,0:T(8,128)S(1)} %add_add_fusion.refs_0_), channel_id=1, source_target_pairs={{0,16},{4,20},{8,24},{12,28},{16,0},{20,4},{24,8},{28,12},{1,17},{... | collective-permute-start | bytes 61448 | tf_op jit(solution)/shard_map/ppermute | solution.py:316
  60.0 2.1 %collective-permute-done.15.refs_1_ = f32[40,128]{1,0:T(8,128)S(1)} collective-permute-done((f32[40,128]{1,0:T(8,128)S(1)}, f32[40,128]{1,0:T(8,128)S(1)}, u32[]{:S(2)}, u32[]{:S(2)}) %collective-permute-start.15) | collective-permute-done | bytes 20512 | tf_op jit(solution)/shard_map/ppermute | solution.py:316
  62.1 0.0 copy-done
  62.1 0.6 copy-done.13
  62.7 1.7 %final.1 = (f32[2,10,4,62]{3,2,1,0:T(4,128)}, f32[2,10,4,62]{3,2,1,0:T(4,128)}) custom-call(s32[1]{0:T(128)} %bitcast.offset_ref, f32[10]{0:T(128)} %rho_ref.11, f32[40,128]{1,0:T(8,128)} %copy-done, f32[40,128]{1,0:T(8,128)} %copy-done.13, f32[40,128]{1,0:T(8,128)} %get-tuple-element.30.refs_2_, f32[2,10,4,62]{3,2,1,0:T(4,128)} %bitcast.9), custom_call_target="tpu_custom_call" | custom-call | tf_op jit(solution)/shard_map/final/pallas_call | solution.py:413
  (4 shorter events, 0.0 us)
Async XLA Ops:
  8.8 4.6 %collective-permute-start.2 = (f32[64,128]{1,0:T(8,128)}, f32[64,128]{1,0:T(8,128)S(1)}, u32[]{:S(2)}, u32[]{:S(2)}) collective-permute-start(f32[64,128]{1,0:T(8,128)} %get-tuple-element.18.refs_0_), channel_id=1, source_target_pairs={{0,3},{1,2},{2,1},{3,0},{4,7},{5,6},{6,5},{7,4},{8,11},{9,10},{10,... | collective-permute-start | bytes 98312 | tf_op jit(solution)/shard_map/ppermute | solution.py:316
  11.3 4.2 %collective-permute-start.1 = (f32[64,128]{1,0:T(8,128)}, f32[64,128]{1,0:T(8,128)S(1)}, u32[]{:S(2)}, u32[]{:S(2)}) collective-permute-start(f32[64,128]{1,0:T(8,128)} %get-tuple-element.18.refs_0_), channel_id=1, source_target_pairs={{0,2},{1,3},{2,0},{3,1},{4,6},{5,7},{6,4},{7,5},{8,10},{9,11},{10,... | collective-permute-start | bytes 98312 | tf_op jit(solution)/shard_map/ppermute | solution.py:316
  11.9 3.5 %collective-permute-start = (f32[64,128]{1,0:T(8,128)}, f32[64,128]{1,0:T(8,128)S(1)}, u32[]{:S(2)}, u32[]{:S(2)}) collective-permute-start(f32[64,128]{1,0:T(8,128)} %get-tuple-element.18.refs_0_), channel_id=1, source_target_pairs={{0,1},{1,0},{2,3},{3,2},{4,5},{5,4},{6,7},{7,6},{8,9},{9,8},{10,11... | collective-permute-start | bytes 98312 | tf_op jit(solution)/shard_map/ppermute | solution.py:316
  13.4 2.1 %copy-start.2 = (f32[64,128]{1,0:T(8,128)}, f32[64,128]{1,0:T(8,128)S(1)}, u32[]{:S(2)}) copy-start(f32[64,128]{1,0:T(8,128)S(1)} %collective-permute-done.2.refs_3_) | copy-start | bytes 98308
  15.5 0.6 copy-start.5
  15.5 0.6 copy-start.8
  21.4 3.9 %collective-permute-start.5 = (f32[64,128]{1,0:T(8,128)}, f32[64,128]{1,0:T(8,128)S(1)}, u32[]{:S(2)}, u32[]{:S(2)}) collective-permute-start(f32[64,128]{1,0:T(8,128)} %get-tuple-element.22.refs_0_), channel_id=1, source_target_pairs={{0,3},{1,2},{2,1},{3,0},{4,7},{5,6},{6,5},{7,4},{8,11},{9,10},{10,... | collective-permute-start | bytes 98312 | tf_op jit(solution)/shard_map/ppermute | solution.py:316
  22.1 4.1 %collective-permute-start.4 = (f32[64,128]{1,0:T(8,128)}, f32[64,128]{1,0:T(8,128)S(1)}, u32[]{:S(2)}, u32[]{:S(2)}) collective-permute-start(f32[64,128]{1,0:T(8,128)} %get-tuple-element.22.refs_0_), channel_id=1, source_target_pairs={{0,2},{1,3},{2,0},{3,1},{4,6},{5,7},{6,4},{7,5},{8,10},{9,11},{10,... | collective-permute-start | bytes 98312 | tf_op jit(solution)/shard_map/ppermute | solution.py:316
  22.9 3.4 %collective-permute-start.3 = (f32[64,128]{1,0:T(8,128)}, f32[64,128]{1,0:T(8,128)S(1)}, u32[]{:S(2)}, u32[]{:S(2)}) collective-permute-start(f32[64,128]{1,0:T(8,128)} %get-tuple-element.22.refs_0_), channel_id=1, source_target_pairs={{0,1},{1,0},{2,3},{3,2},{4,5},{5,4},{6,7},{7,6},{8,9},{9,8},{10,11... | collective-permute-start | bytes 98312 | tf_op jit(solution)/shard_map/ppermute | solution.py:316
  25.3 0.9 %copy-start.3 = (f32[64,128]{1,0:T(8,128)}, f32[64,128]{1,0:T(8,128)S(1)}, u32[]{:S(2)}) copy-start(f32[64,128]{1,0:T(8,128)S(1)} %collective-permute-done.5.refs_3_) | copy-start | bytes 98308
  26.2 0.6 copy-start.6
  26.2 0.6 copy-start.9
  32.2 3.6 %collective-permute-start.8 = (f32[64,128]{1,0:T(8,128)}, f32[64,128]{1,0:T(8,128)S(1)}, u32[]{:S(2)}, u32[]{:S(2)}) collective-permute-start(f32[64,128]{1,0:T(8,128)} %get-tuple-element.24.refs_0_), channel_id=1, source_target_pairs={{0,3},{1,2},{2,1},{3,0},{4,7},{5,6},{6,5},{7,4},{8,11},{9,10},{10,... | collective-permute-start | bytes 98312 | tf_op jit(solution)/shard_map/ppermute | solution.py:316
  32.5 4.2 %collective-permute-start.7 = (f32[64,128]{1,0:T(8,128)}, f32[64,128]{1,0:T(8,128)S(1)}, u32[]{:S(2)}, u32[]{:S(2)}) collective-permute-start(f32[64,128]{1,0:T(8,128)} %get-tuple-element.24.refs_0_), channel_id=1, source_target_pairs={{0,2},{1,3},{2,0},{3,1},{4,6},{5,7},{6,4},{7,5},{8,10},{9,11},{10,... | collective-permute-start | bytes 98312 | tf_op jit(solution)/shard_map/ppermute | solution.py:316
  33.1 3.6 %collective-permute-start.6 = (f32[64,128]{1,0:T(8,128)}, f32[64,128]{1,0:T(8,128)S(1)}, u32[]{:S(2)}, u32[]{:S(2)}) collective-permute-start(f32[64,128]{1,0:T(8,128)} %get-tuple-element.24.refs_0_), channel_id=1, source_target_pairs={{0,1},{1,0},{2,3},{3,2},{4,5},{5,4},{6,7},{7,6},{8,9},{9,8},{10,11... | collective-permute-start | bytes 98312 | tf_op jit(solution)/shard_map/ppermute | solution.py:316
  35.7 0.9 %copy-start.1 = (f32[64,128]{1,0:T(8,128)}, f32[64,128]{1,0:T(8,128)S(1)}, u32[]{:S(2)}) copy-start(f32[64,128]{1,0:T(8,128)S(1)} %collective-permute-done.8.refs_3_) | copy-start | bytes 98308
  36.6 0.6 copy-start.4
  36.6 0.6 copy-start.7
  42.6 3.9 %collective-permute-start.11 = (f32[64,128]{1,0:T(8,128)}, f32[64,128]{1,0:T(8,128)S(1)}, u32[]{:S(2)}, u32[]{:S(2)}) collective-permute-start(f32[64,128]{1,0:T(8,128)} %get-tuple-element.26.refs_0_), channel_id=1, source_target_pairs={{0,3},{1,2},{2,1},{3,0},{4,7},{5,6},{6,5},{7,4},{8,11},{9,10},{10,... | collective-permute-start | bytes 98312 | tf_op jit(solution)/shard_map/ppermute | solution.py:316
  43.1 4.1 %collective-permute-start.10 = (f32[64,128]{1,0:T(8,128)}, f32[64,128]{1,0:T(8,128)S(1)}, u32[]{:S(2)}, u32[]{:S(2)}) collective-permute-start(f32[64,128]{1,0:T(8,128)} %get-tuple-element.26.refs_0_), channel_id=1, source_target_pairs={{0,2},{1,3},{2,0},{3,1},{4,6},{5,7},{6,4},{7,5},{8,10},{9,11},{10,... | collective-permute-start | bytes 98312 | tf_op jit(solution)/shard_map/ppermute | solution.py:316
  44.0 3.2 %collective-permute-start.9 = (f32[64,128]{1,0:T(8,128)}, f32[64,128]{1,0:T(8,128)S(1)}, u32[]{:S(2)}, u32[]{:S(2)}) collective-permute-start(f32[64,128]{1,0:T(8,128)} %get-tuple-element.26.refs_0_), channel_id=1, source_target_pairs={{0,1},{1,0},{2,3},{3,2},{4,5},{5,4},{6,7},{7,6},{8,9},{9,8},{10,11... | collective-permute-start | bytes 98312 | tf_op jit(solution)/shard_map/ppermute | solution.py:316
  46.5 0.7 %copy-start.10 = (f32[64,128]{1,0:T(8,128)}, f32[64,128]{1,0:T(8,128)S(1)}, u32[]{:S(2)}) copy-start(f32[64,128]{1,0:T(8,128)S(1)} %collective-permute-done.11.refs_3_) | copy-start | bytes 98308
  47.2 0.6 copy-start.11
  47.2 0.6 copy-start.12
  49.6 5.0 %collective-permute-start.14 = (f32[40,128]{1,0:T(8,128)}, f32[40,128]{1,0:T(8,128)S(1)}, u32[]{:S(2)}, u32[]{:S(2)}) collective-permute-start(f32[40,128]{1,0:T(8,128)} %get-tuple-element.29), channel_id=1, source_target_pairs={{0,12},{4,8},{8,4},{12,0},{16,28},{20,24},{24,20},{28,16},{1,13},{... | collective-permute-start | bytes 61448 | tf_op jit(solution)/shard_map/ppermute | solution.py:316
  52.1 4.0 %collective-permute-start.13 = (f32[40,128]{1,0:T(8,128)}, f32[40,128]{1,0:T(8,128)S(1)}, u32[]{:S(2)}, u32[]{:S(2)}) collective-permute-start(f32[40,128]{1,0:T(8,128)} %get-tuple-element.29), channel_id=1, source_target_pairs={{0,8},{4,12},{8,0},{12,4},{16,24},{20,28},{24,16},{28,20},{1,9},{5... | collective-permute-start | bytes 61448 | tf_op jit(solution)/shard_map/ppermute | solution.py:316
  52.6 4.0 %collective-permute-start.12 = (f32[40,128]{1,0:T(8,128)}, f32[40,128]{1,0:T(8,128)S(1)}, u32[]{:S(2)}, u32[]{:S(2)}) collective-permute-start(f32[40,128]{1,0:T(8,128)} %get-tuple-element.29), channel_id=1, source_target_pairs={{0,4},{4,0},{8,12},{12,8},{16,20},{20,16},{24,28},{28,24},{1,5},{5... | collective-permute-start | bytes 61448 | tf_op jit(solution)/shard_map/ppermute | solution.py:316
  57.3 4.7 %copy-start = (f32[40,128]{1,0:T(8,128)}, f32[40,128]{1,0:T(8,128)S(1)}, u32[]{:S(2)}) copy-start(f32[40,128]{1,0:T(8,128)S(1)} %add_add_fusion.refs_0_) | copy-start | bytes 61444
  57.3 4.7 %collective-permute-start.15 = (f32[40,128]{1,0:T(8,128)S(1)}, f32[40,128]{1,0:T(8,128)S(1)}, u32[]{:S(2)}, u32[]{:S(2)}) collective-permute-start(f32[40,128]{1,0:T(8,128)S(1)} %add_add_fusion.refs_0_), channel_id=1, source_target_pairs={{0,16},{4,20},{8,24},{12,28},{16,0},{20,4},{24,8},{28,12},{1,17},{... | collective-permute-start | bytes 61448 | tf_op jit(solution)/shard_map/ppermute | solution.py:316
  62.1 0.6 copy-start.13

commit v2 on v1

--- a/solution.py
+++ b/solution.py
@@ -170,7 +170,7 @@
     )
 
 
-def sweep_block(gains, pairs_ref, tiles, per, times, tile_ref, at_ref, by_first, by_second):
+def sweep_block(gains, pairs_ref, tiles, per, times, tile_ref, at_ref, by_first, by_second, waits=()):
     rows = gains.shape[0]
     left = gather_rows(gains)
     pairs = pairs_ref[...]
@@ -185,7 +185,11 @@
         sweep_tile(j, per, times, tile_ref, at_ref, by_first, by_second)
         return carry
 
-    lax.fori_loop(0, tiles, step, 0)
+    blocks = max(len(waits), 1)
+    for b in range(blocks):
+        if waits:
+            waits[b].wait()
+        lax.fori_loop(b * tiles // blocks, (b + 1) * tiles // blocks, step, 0, unroll=True)
     across = (((1,), (1,)), ((), ()))
     sums = 0.0
     for ref, choice in ((by_first, first), (by_second, second)):
@@ -208,8 +212,8 @@
 
 
 def opening_kernel(
-    sizes, offset_ref, rho_ref, coh_in, vis_in, pairs_ref, gains_in, duals_in, cons_in,
-    tile_ref, gains_ref, target_ref, sums_ref,
+    sizes, offset_ref, rho_ref, coh_in, vis_in, pairs_in, gains_in, duals_in, cons_in,
+    tile_ref, pairs_ref, gains_ref, target_ref, sums_ref,
     acc_ref, pad_ref, at_ref, by_first, by_second,
 ):
     per, times, total, count, pairs_count, tiles = sizes
@@ -231,6 +235,10 @@
         target_ref[...] = rho_rows(rho_ref, rows, per) * prior - target_ref[...]
         acc_ref[...] = jnp.zeros(acc_ref.shape, jnp.float32)
 
+    width = tiles * LANES
+    inside = step * width + lax.broadcasted_iota(jnp.int32, (2, width), 1) < pairs_count
+    pairs_ref[0:2, :] = jnp.where(inside, pairs_in[...], -1)
+    pairs_ref[2:8, :] = jnp.full((6, width), -1, jnp.int32)
     for j in range(tiles):
         lanes = slice(j * LANES, (j + 1) * LANES)
         place = (step * tiles + j) * LANES + lax.broadcasted_iota(jnp.int32, (times, LANES), 1)
@@ -262,19 +270,26 @@
 def sweep_kernel(sizes, ways, rho_ref, *refs):
     per, times, total, count, pairs_count, tiles = sizes
     parts = refs[:ways]
-    gains_in, target_ref, tile_ref, pairs_ref, gains_ref, sums_ref = refs[ways:ways + 6]
-    at_ref, by_first, by_second = refs[ways + 6:]
+    gains_in, target_ref, tile_any, pairs_ref, gains_ref, sums_ref = refs[ways:ways + 6]
+    tile_ref, arrived, at_ref, by_first, by_second = refs[ways + 6:]
     rows = gains_in.shape[0]
+    all_tiles = tile_ref.shape[0]
+    copies = [
+        pltpu.make_async_copy(
+            tile_any.at[pl.ds(b * tiles, tiles)], tile_ref.at[pl.ds(b * tiles, tiles)], arrived.at[b]
+        )
+        for b in range(all_tiles // tiles)
+    ]
+    for copy in copies:
+        copy.start()
     gains = refine(
         total_of([part[...] for part in parts]), gains_in[...], target_ref[...], rho_rows(rho_ref, rows, per)
     )
     gains_ref[...] = gains
-    sums_ref[...] = join(
-        sweep_block(
-            gains, pairs_ref, tile_ref.shape[0], per, times, tile_ref, at_ref, by_first, by_second
-        ),
-        rows,
-    )
+    sums = sweep_block(
+        gains, pairs_ref, all_tiles, per, times, tile_ref, at_ref, by_first, by_second, copies
+    )
+    sums_ref[...] = join(sums, rows)
 
 
 def closing_kernel(sizes, terms, ways, offset_ref, rho_ref, *refs):
@@ -335,7 +350,6 @@
     tiles = max(d for d in range(1, 6) if all_tiles % d == 0)
     steps = all_tiles // tiles
     width = tiles * LANES
-    pairs = jnp.pad(pairs, ((0, 8 - pairs.shape[0]), (0, all_tiles * LANES - pairs_count)), constant_values=-1)
     gains = jnp.swapaxes(gains, 1, 2)
     duals = jnp.swapaxes(duals, 1, 2)
     consensus = jnp.swapaxes(consensus, 1, 2)
@@ -351,7 +365,7 @@
             pltpu.VMEM((blocks, 6 * rows, LANES), jnp.bfloat16),
         ]
 
-    tile_data, gains_now, target, sums = pl.pallas_call(
+    tile_data, marked, gains_now, target, sums = pl.pallas_call(
         functools.partial(opening_kernel, sizes),
         name="opening",
         grid=(steps,),
@@ -360,19 +374,21 @@
             smem,
             pl.BlockSpec((directions, 2, per, times, width), lambda i: (0, 0, 0, 0, i)),
             pl.BlockSpec((2, per, times, width), lambda i: (0, 0, 0, i)),
-            pl.BlockSpec((8, width), lambda i: (0, i)),
+            pl.BlockSpec((2, width), lambda i: (0, i)),
             pl.BlockSpec(gains.shape, lambda i: (0, 0, 0, 0)),
             pl.BlockSpec(duals.shape, lambda i: (0, 0, 0, 0)),
             pl.BlockSpec(consensus.shape, lambda i: (0, 0, 0, 0)),
         ],
         out_specs=[
             pl.BlockSpec((tiles, height, LANES), lambda i: (i, 0, 0)),
+            pl.BlockSpec((8, width), lambda i: (0, i)),
             pl.BlockSpec((rows, LANES), lambda i: (0, 0)),
             pl.BlockSpec((rows, LANES), lambda i: (0, 0)),
             pl.BlockSpec((sum_rows, LANES), lambda i: (0, 0)),
         ],
         out_shape=[
             shape_of(all_tiles, height, LANES),
+            shape_of(8, all_tiles * LANES, dtype=jnp.int32),
             packed,
             packed,
             shape_of(sum_rows, LANES),
@@ -389,11 +405,15 @@
         gains_now, sums = pl.pallas_call(
             functools.partial(sweep_kernel, sizes, ways),
             name="sweep",
-            in_specs=[smem] + [vmem] * (ways + 4),
+            in_specs=[smem] + [vmem] * (ways + 2) + [pl.BlockSpec(memory_space=pl.ANY), vmem],
             out_specs=[vmem, vmem],
             out_shape=[packed, shape_of(sum_rows, LANES)],
-            scratch_shapes=work(all_tiles),
-        )(rho, *exchange(sums, "tm", peers), gains_now, target, tile_data, pairs)
+            scratch_shapes=[
+                pltpu.VMEM((all_tiles, height, LANES), jnp.float32),
+                pltpu.SemaphoreType.DMA((steps,)),
+            ]
+            + work(all_tiles),
+        )(rho, *exchange(sums, "tm", peers), gains_now, target, tile_data, marked)
 
     gains_now, solved, fit = pl.pallas_call(
         functools.partial(closing_kernel, sizes, terms, ways),

time: 64.8 us -> 61.6 us (0.951)
  Pallas kernels: 26.3 us -> 24.1 us
  local copies, waits for them, and re-layouts: 4.42 us -> 3.07 us
    pallas_call x3, Pallas kernels: 16 us -> 13.9 us  [local(): pl.pallas_call(functools.partial(sweep_kernel, sizes, ways), name='sweep'...]
    pad x1 -> x0, local copies, waits for them, and re-layouts: 1.35 us -> none  [local(): jnp.pad(pairs, ((0, 8 - pairs.shape[0]), (0, all_tiles * LANES - pairs_co...]
where the time goes in v2:
time: 61.6 us; the launch traced here: 61 us
  Pallas kernels  24.1 us (39%)
  waiting for transfers between devices  17.3 us (28%)
  starting transfers between devices  15.1 us (25%)
  local copies, waits for them, and re-layouts  3.07 us (5%)
  other arithmetic  0.73 us (1%)
  between operations  0.71 us (1%)
    ppermute x16, waiting for transfers between devices, exchange(): lax.ppermute(x, axis, [(i, i ^ s) for i in range(count)])  17.3 us
    ppermute x16, starting transfers between devices, exchange(): lax.ppermute(x, axis, [(i, i ^ s) for i in range(count)])  15.1 us
    pallas_call x3, Pallas kernels, local(): pl.pallas_call(functools.partial(sweep_kernel, sizes, ways), name='sweep'...  13.9 us
    pallas_call x1, Pallas kernels, local(): pl.pallas_call(functools.partial(opening_kernel, sizes), name='opening',...  6.59 us
    unnamed x28, local copies, waits for them, and re-layouts  3.07 us
    pallas_call x1, Pallas kernels, local(): pl.pallas_call(functools.partial(closing_kernel, sizes, terms, ways), nam...  1.81 us
    pallas_call x1, Pallas kernels, local(): pl.pallas_call(functools.partial(final_kernel, sizes, len(parts)), name='...  1.73 us
  transfers between devices with their start and end apart: 16, of which 12 were waited for; matrix products, arithmetic and copies ran while one was open for 0% of the time, Pallas kernels for 0%

profile of v2, /device:TPU:0, one launch (start us, length us, event | category | flops | bytes accessed | tf_op | source)
XLA Modules:
  0.0 61.0 jit_solution(13853523602767403259)
XLA Ops:
  0.6 6.6 %opening.1 = (f32[15,480,128]{2,1,0:T(8,128)}, s32[8,1920]{1,0:T(8,128)}, f32[40,128]{1,0:T(8,128)}, f32[40,128]{1,0:T(8,128)}, f32[64,128]{1,0:T(8,128)}) custom-call(s32[1]{0:T(128)} %bitcast.offset_ref, f32[10]{0:T(128)} %rho_ref.11, f32[10,2,4,4,1891]{4,3,2,1,0:T(4,128)} %coh_in.1, f32[2,4,4,1891]{3,2,1,0:T(4,128)} %vis_in.1, s32[2,1891]{1,0:T(2,128)} %pairs_in.1, ...), custom_call_target="tpu_custom_call" | custom-call | tf_op jit(solution)/shard_map/opening/pallas_call | solution.py:368
  7.2 2.5 %collective-permute-start.2 = (f32[64,128]{1,0:T(8,128)}, f32[64,128]{1,0:T(8,128)S(1)}, u32[]{:S(2)}, u32[]{:S(2)}) collective-permute-start(f32[64,128]{1,0:T(8,128)} %get-tuple-element.19.refs_0_), channel_id=1, source_target_pairs={{0,3},{1,2},{2,1},{3,0},{4,7},{5,6},{6,5},{7,4},{8,11},{9,10},{10,... | collective-permute-start | bytes 98312 | tf_op jit(solution)/shard_map/ppermute | solution.py:331
  9.7 0.6 %collective-permute-start.1 = (f32[64,128]{1,0:T(8,128)}, f32[64,128]{1,0:T(8,128)S(1)}, u32[]{:S(2)}, u32[]{:S(2)}) collective-permute-start(f32[64,128]{1,0:T(8,128)} %get-tuple-element.19.refs_0_), channel_id=1, source_target_pairs={{0,2},{1,3},{2,0},{3,1},{4,6},{5,7},{6,4},{7,5},{8,10},{9,11},{10,... | collective-permute-start | bytes 98312 | tf_op jit(solution)/shard_map/ppermute | solution.py:331
  10.4 0.0 collective-permute-start
  10.4 1.4 %collective-permute-done.2.refs_3_ = f32[64,128]{1,0:T(8,128)S(1)} collective-permute-done((f32[64,128]{1,0:T(8,128)}, f32[64,128]{1,0:T(8,128)S(1)}, u32[]{:S(2)}, u32[]{:S(2)}) %collective-permute-start.2) | collective-permute-done | bytes 32800 | tf_op jit(solution)/shard_map/ppermute | solution.py:331
  11.8 0.0 copy-start.2
  11.8 2.1 %collective-permute-done.1.refs_2_ = f32[64,128]{1,0:T(8,128)S(1)} collective-permute-done((f32[64,128]{1,0:T(8,128)}, f32[64,128]{1,0:T(8,128)S(1)}, u32[]{:S(2)}, u32[]{:S(2)}) %collective-permute-start.1) | collective-permute-done | bytes 32800 | tf_op jit(solution)/shard_map/ppermute | solution.py:331
  13.9 0.0 copy-start.5
  13.9 0.0 collective-permute-done.refs_1_
  13.9 0.0 copy-start.8
  13.9 0.0 copy-done.2
  13.9 0.6 copy-done.5
  14.5 0.0 copy-done.8
  14.5 4.7 %sweep.3 = (f32[40,128]{1,0:T(8,128)}, f32[64,128]{1,0:T(8,128)}) custom-call(f32[10]{0:T(128)} %rho_ref.11, f32[64,128]{1,0:T(8,128)} %get-tuple-element.19.refs_0_, f32[64,128]{1,0:T(8,128)} %copy-done.8, f32[64,128]{1,0:T(8,128)} %copy-done.5, f32[64,128]{1,0:T(8,128)} %copy-done.2, f32[40,128]{1,0:T(8,128)} %get-tuple-element.20.refs_4_, ...), custom_call_target="tpu_custom_call" | custom-call | tf_op jit(solution)/shard_map/sweep/pallas_call | solution.py:405
  19.2 0.7 %collective-permute-start.5 = (f32[64,128]{1,0:T(8,128)}, f32[64,128]{1,0:T(8,128)S(1)}, u32[]{:S(2)}, u32[]{:S(2)}) collective-permute-start(f32[64,128]{1,0:T(8,128)} %get-tuple-element.24.refs_0_), channel_id=1, source_target_pairs={{0,3},{1,2},{2,1},{3,0},{4,7},{5,6},{6,5},{7,4},{8,11},{9,10},{10,... | collective-permute-start | bytes 98312 | tf_op jit(solution)/shard_map/ppermute | solution.py:331
  20.0 0.8 %collective-permute-start.4 = (f32[64,128]{1,0:T(8,128)}, f32[64,128]{1,0:T(8,128)S(1)}, u32[]{:S(2)}, u32[]{:S(2)}) collective-permute-start(f32[64,128]{1,0:T(8,128)} %get-tuple-element.24.refs_0_), channel_id=1, source_target_pairs={{0,2},{1,3},{2,0},{3,1},{4,6},{5,7},{6,4},{7,5},{8,10},{9,11},{10,... | collective-permute-start | bytes 98312 | tf_op jit(solution)/shard_map/ppermute | solution.py:331
  20.7 0.4 collective-permute-start.3
  21.1 2.0 %collective-permute-done.5.refs_3_ = f32[64,128]{1,0:T(8,128)S(1)} collective-permute-done((f32[64,128]{1,0:T(8,128)}, f32[64,128]{1,0:T(8,128)S(1)}, u32[]{:S(2)}, u32[]{:S(2)}) %collective-permute-start.5) | collective-permute-done | bytes 32800 | tf_op jit(solution)/shard_map/ppermute | solution.py:331
  23.2 0.0 copy-start.3
  23.2 0.9 %collective-permute-done.4.refs_2_ = f32[64,128]{1,0:T(8,128)S(1)} collective-permute-done((f32[64,128]{1,0:T(8,128)}, f32[64,128]{1,0:T(8,128)S(1)}, u32[]{:S(2)}, u32[]{:S(2)}) %collective-permute-start.4) | collective-permute-done | bytes 32800 | tf_op jit(solution)/shard_map/ppermute | solution.py:331
  24.1 0.0 copy-start.6
  24.1 0.0 collective-permute-done.3.refs_1_
  24.1 0.0 copy-start.9
  24.1 0.0 copy-done.3
  24.1 0.6 copy-done.6
  24.7 0.0 copy-done.9
  24.7 4.6 %sweep.4 = (f32[40,128]{1,0:T(8,128)}, f32[64,128]{1,0:T(8,128)}) custom-call(f32[10]{0:T(128)} %rho_ref.11, f32[64,128]{1,0:T(8,128)} %get-tuple-element.24.refs_0_, f32[64,128]{1,0:T(8,128)} %copy-done.9, f32[64,128]{1,0:T(8,128)} %copy-done.6, f32[64,128]{1,0:T(8,128)} %copy-done.3, f32[40,128]{1,0:T(8,128)} %get-tuple-element.25.refs_4_, ...), custom_call_target="tpu_custom_call" | custom-call | tf_op jit(solution)/shard_map/sweep/pallas_call | solution.py:405
  29.4 0.3 collective-permute-start.8
  29.7 0.6 %collective-permute-start.7 = (f32[64,128]{1,0:T(8,128)}, f32[64,128]{1,0:T(8,128)S(1)}, u32[]{:S(2)}, u32[]{:S(2)}) collective-permute-start(f32[64,128]{1,0:T(8,128)} %get-tuple-element.26.refs_0_), channel_id=1, source_target_pairs={{0,2},{1,3},{2,0},{3,1},{4,6},{5,7},{6,4},{7,5},{8,10},{9,11},{10,... | collective-permute-start | bytes 98312 | tf_op jit(solution)/shard_map/ppermute | solution.py:331
  30.3 0.9 %collective-permute-start.6 = (f32[64,128]{1,0:T(8,128)}, f32[64,128]{1,0:T(8,128)S(1)}, u32[]{:S(2)}, u32[]{:S(2)}) collective-permute-start(f32[64,128]{1,0:T(8,128)} %get-tuple-element.26.refs_0_), channel_id=1, source_target_pairs={{0,1},{1,0},{2,3},{3,2},{4,5},{5,4},{6,7},{7,6},{8,9},{9,8},{10,11... | collective-permute-start | bytes 98312 | tf_op jit(solution)/shard_map/ppermute | solution.py:331
  31.3 1.7 %collective-permute-done.8.refs_3_ = f32[64,128]{1,0:T(8,128)S(1)} collective-permute-done((f32[64,128]{1,0:T(8,128)}, f32[64,128]{1,0:T(8,128)S(1)}, u32[]{:S(2)}, u32[]{:S(2)}) %collective-permute-start.8) | collective-permute-done | bytes 32800 | tf_op jit(solution)/shard_map/ppermute | solution.py:331
  33.0 0.0 copy-start.1
  33.0 0.9 %collective-permute-done.7.refs_2_ = f32[64,128]{1,0:T(8,128)S(1)} collective-permute-done((f32[64,128]{1,0:T(8,128)}, f32[64,128]{1,0:T(8,128)S(1)}, u32[]{:S(2)}, u32[]{:S(2)}) %collective-permute-start.7) | collective-permute-done | bytes 32800 | tf_op jit(solution)/shard_map/ppermute | solution.py:331
  33.9 0.0 copy-start.4
  33.9 0.0 collective-permute-done.6.refs_1_
  33.9 0.0 copy-start.7
  33.9 0.0 copy-done.1
  33.9 0.6 copy-done.4
  34.5 0.0 copy-done.7
  34.5 4.6 %sweep.5 = (f32[40,128]{1,0:T(8,128)}, f32[64,128]{1,0:T(8,128)}) custom-call(f32[10]{0:T(128)} %rho_ref.11, f32[64,128]{1,0:T(8,128)} %get-tuple-element.26.refs_0_, f32[64,128]{1,0:T(8,128)} %copy-done.7, f32[64,128]{1,0:T(8,128)} %copy-done.4, f32[64,128]{1,0:T(8,128)} %copy-done.1, f32[40,128]{1,0:T(8,128)} %get-tuple-element.27.refs_4_, ...), custom_call_target="tpu_custom_call" | custom-call | tf_op jit(solution)/shard_map/sweep/pallas_call | solution.py:405
  39.2 0.6 collective-permute-start.11
  39.7 1.0 %collective-permute-start.10 = (f32[64,128]{1,0:T(8,128)}, f32[64,128]{1,0:T(8,128)S(1)}, u32[]{:S(2)}, u32[]{:S(2)}) collective-permute-start(f32[64,128]{1,0:T(8,128)} %get-tuple-element.28.refs_0_), channel_id=1, source_target_pairs={{0,2},{1,3},{2,0},{3,1},{4,6},{5,7},{6,4},{7,5},{8,10},{9,11},{10,... | collective-permute-start | bytes 98312 | tf_op jit(solution)/shard_map/ppermute | solution.py:331
  40.7 0.4 collective-permute-start.9
  41.1 2.0 %collective-permute-done.11.refs_3_ = f32[64,128]{1,0:T(8,128)S(1)} collective-permute-done((f32[64,128]{1,0:T(8,128)}, f32[64,128]{1,0:T(8,128)S(1)}, u32[]{:S(2)}, u32[]{:S(2)}) %collective-permute-start.11) | collective-permute-done | bytes 32800 | tf_op jit(solution)/shard_map/ppermute | solution.py:331
  43.1 0.0 copy-start.10
  43.1 0.7 %collective-permute-done.10.refs_2_ = f32[64,128]{1,0:T(8,128)S(1)} collective-permute-done((f32[64,128]{1,0:T(8,128)}, f32[64,128]{1,0:T(8,128)S(1)}, u32[]{:S(2)}, u32[]{:S(2)}) %collective-permute-start.10) | collective-permute-done | bytes 32800 | tf_op jit(solution)/shard_map/ppermute | solution.py:331
  43.9 0.0 copy-start.11
  43.9 0.0 collective-permute-done.9.refs_1_
  43.9 0.0 copy-done.10
  43.9 0.6 copy-done.11
  44.5 0.0 copy-done.12
  44.5 1.8 %closing.1 = (f32[40,128]{1,0:T(8,128)}, f32[2,10,4,62]{3,2,1,0:T(4,128)}, f32[40,128]{1,0:T(8,128)}) custom-call(s32[1]{0:T(128)} %bitcast.offset_ref, f32[10]{0:T(128)} %rho_ref.11, f32[64,128]{1,0:T(8,128)} %get-tuple-element.28.refs_0_, f32[64,128]{1,0:T(8,128)} %copy-done.12, f32[64,128]{1,0:T(8,128)} %copy-done.11, f32[64,128]{1,0:T(8,128)} %copy-done.10, ...), custom_call_target="tpu_custom_call" | custom-call | tf_op jit(solution)/shard_map/closing/pallas_call | solution.py:418
  46.3 2.5 %collective-permute-start.14 = (f32[40,128]{1,0:T(8,128)}, f32[40,128]{1,0:T(8,128)S(1)}, u32[]{:S(2)}, u32[]{:S(2)}) collective-permute-start(f32[40,128]{1,0:T(8,128)} %get-tuple-element.31), channel_id=1, source_target_pairs={{0,12},{4,8},{8,4},{12,0},{16,28},{20,24},{24,20},{28,16},{1,13},{... | collective-permute-start | bytes 61448 | tf_op jit(solution)/shard_map/ppermute | solution.py:331
  48.8 0.4 collective-permute-start.13
  49.2 0.6 collective-permute-start.12
  49.8 1.5 %collective-permute-done.14 = f32[40,128]{1,0:T(8,128)S(1)} collective-permute-done((f32[40,128]{1,0:T(8,128)}, f32[40,128]{1,0:T(8,128)S(1)}, u32[]{:S(2)}, u32[]{:S(2)}) %collective-permute-start.14) | collective-permute-done | bytes 20512 | tf_op jit(solution)/shard_map/ppermute | solution.py:331
  51.3 1.5 %collective-permute-done.13 = f32[40,128]{1,0:T(8,128)S(1)} collective-permute-done((f32[40,128]{1,0:T(8,128)}, f32[40,128]{1,0:T(8,128)S(1)}, u32[]{:S(2)}, u32[]{:S(2)}) %collective-permute-start.13) | collective-permute-done | bytes 20512 | tf_op jit(solution)/shard_map/ppermute | solution.py:331
  52.8 0.4 collective-permute-done.12
  53.2 0.7 %add_add_fusion.refs_0_ = f32[40,128]{1,0:T(8,128)S(1)} fusion(f32[40,128]{1,0:T(8,128)S(1)} %collective-permute-done.13, f32[40,128]{1,0:T(8,128)S(1)} %collective-permute-done.14, f32[40,128]{1,0:T(8,128)} %get-tuple-element.31, f32[40,128]{1,0:T(8,128)S(1)} %collective-permute-done.12), kind=kLoop, calls=%fused_computation | loop fusion | flops 15360 | bytes 102400 | tf_op jit(solution)/shard_map/add | solution.py:87
  54.0 2.7 %collective-permute-start.15 = (f32[40,128]{1,0:T(8,128)S(1)}, f32[40,128]{1,0:T(8,128)S(1)}, u32[]{:S(2)}, u32[]{:S(2)}) collective-permute-start(f32[40,128]{1,0:T(8,128)S(1)} %add_add_fusion.refs_0_), channel_id=1, source_target_pairs={{0,16},{4,20},{8,24},{12,28},{16,0},{20,4},{24,8},{28,12},{1,17},{... | collective-permute-start | bytes 61448 | tf_op jit(solution)/shard_map/ppermute | solution.py:331
  56.6 2.1 %collective-permute-done.15.refs_1_ = f32[40,128]{1,0:T(8,128)S(1)} collective-permute-done((f32[40,128]{1,0:T(8,128)S(1)}, f32[40,128]{1,0:T(8,128)S(1)}, u32[]{:S(2)}, u32[]{:S(2)}) %collective-permute-start.15) | collective-permute-done | bytes 20512 | tf_op jit(solution)/shard_map/ppermute | solution.py:331
  58.7 0.0 copy-done
  58.7 0.6 copy-done.13
  59.3 1.7 %final.1 = (f32[2,10,4,62]{3,2,1,0:T(4,128)}, f32[2,10,4,62]{3,2,1,0:T(4,128)}) custom-call(s32[1]{0:T(128)} %bitcast.offset_ref, f32[10]{0:T(128)} %rho_ref.11, f32[40,128]{1,0:T(8,128)} %copy-done, f32[40,128]{1,0:T(8,128)} %copy-done.13, f32[40,128]{1,0:T(8,128)} %get-tuple-element.32.refs_2_, f32[2,10,4,62]{3,2,1,0:T(4,128)} %bitcast.9), custom_call_target="tpu_custom_call" | custom-call | tf_op jit(solution)/shard_map/final/pallas_call | solution.py:433
  (3 shorter events, 0.0 us)
Async XLA Ops:
  7.2 4.6 %collective-permute-start.2 = (f32[64,128]{1,0:T(8,128)}, f32[64,128]{1,0:T(8,128)S(1)}, u32[]{:S(2)}, u32[]{:S(2)}) collective-permute-start(f32[64,128]{1,0:T(8,128)} %get-tuple-element.19.refs_0_), channel_id=1, source_target_pairs={{0,3},{1,2},{2,1},{3,0},{4,7},{5,6},{6,5},{7,4},{8,11},{9,10},{10,... | collective-permute-start | bytes 98312 | tf_op jit(solution)/shard_map/ppermute | solution.py:331
  9.7 4.2 %collective-permute-start.1 = (f32[64,128]{1,0:T(8,128)}, f32[64,128]{1,0:T(8,128)S(1)}, u32[]{:S(2)}, u32[]{:S(2)}) collective-permute-start(f32[64,128]{1,0:T(8,128)} %get-tuple-element.19.refs_0_), channel_id=1, source_target_pairs={{0,2},{1,3},{2,0},{3,1},{4,6},{5,7},{6,4},{7,5},{8,10},{9,11},{10,... | collective-permute-start | bytes 98312 | tf_op jit(solution)/shard_map/ppermute | solution.py:331
  10.4 3.5 %collective-permute-start = (f32[64,128]{1,0:T(8,128)}, f32[64,128]{1,0:T(8,128)S(1)}, u32[]{:S(2)}, u32[]{:S(2)}) collective-permute-start(f32[64,128]{1,0:T(8,128)} %get-tuple-element.19.refs_0_), channel_id=1, source_target_pairs={{0,1},{1,0},{2,3},{3,2},{4,5},{5,4},{6,7},{7,6},{8,9},{9,8},{10,11... | collective-permute-start | bytes 98312 | tf_op jit(solution)/shard_map/ppermute | solution.py:331
  11.8 2.1 %copy-start.2 = (f32[64,128]{1,0:T(8,128)}, f32[64,128]{1,0:T(8,128)S(1)}, u32[]{:S(2)}) copy-start(f32[64,128]{1,0:T(8,128)S(1)} %collective-permute-done.2.refs_3_) | copy-start | bytes 98308
  13.9 0.6 %copy-start.5 = (f32[64,128]{1,0:T(8,128)}, f32[64,128]{1,0:T(8,128)S(1)}, u32[]{:S(2)}) copy-start(f32[64,128]{1,0:T(8,128)S(1)} %collective-permute-done.1.refs_2_) | copy-start | bytes 98308
  13.9 0.6 %copy-start.8 = (f32[64,128]{1,0:T(8,128)}, f32[64,128]{1,0:T(8,128)S(1)}, u32[]{:S(2)}) copy-start(f32[64,128]{1,0:T(8,128)S(1)} %collective-permute-done.refs_1_) | copy-start | bytes 98308
  19.2 4.0 %collective-permute-start.5 = (f32[64,128]{1,0:T(8,128)}, f32[64,128]{1,0:T(8,128)S(1)}, u32[]{:S(2)}, u32[]{:S(2)}) collective-permute-start(f32[64,128]{1,0:T(8,128)} %get-tuple-element.24.refs_0_), channel_id=1, source_target_pairs={{0,3},{1,2},{2,1},{3,0},{4,7},{5,6},{6,5},{7,4},{8,11},{9,10},{10,... | collective-permute-start | bytes 98312 | tf_op jit(solution)/shard_map/ppermute | solution.py:331
  20.0 4.1 %collective-permute-start.4 = (f32[64,128]{1,0:T(8,128)}, f32[64,128]{1,0:T(8,128)S(1)}, u32[]{:S(2)}, u32[]{:S(2)}) collective-permute-start(f32[64,128]{1,0:T(8,128)} %get-tuple-element.24.refs_0_), channel_id=1, source_target_pairs={{0,2},{1,3},{2,0},{3,1},{4,6},{5,7},{6,4},{7,5},{8,10},{9,11},{10,... | collective-permute-start | bytes 98312 | tf_op jit(solution)/shard_map/ppermute | solution.py:331
  20.7 3.4 %collective-permute-start.3 = (f32[64,128]{1,0:T(8,128)}, f32[64,128]{1,0:T(8,128)S(1)}, u32[]{:S(2)}, u32[]{:S(2)}) collective-permute-start(f32[64,128]{1,0:T(8,128)} %get-tuple-element.24.refs_0_), channel_id=1, source_target_pairs={{0,1},{1,0},{2,3},{3,2},{4,5},{5,4},{6,7},{7,6},{8,9},{9,8},{10,11... | collective-permute-start | bytes 98312 | tf_op jit(solution)/shard_map/ppermute | solution.py:331
  23.2 0.9 %copy-start.3 = (f32[64,128]{1,0:T(8,128)}, f32[64,128]{1,0:T(8,128)S(1)}, u32[]{:S(2)}) copy-start(f32[64,128]{1,0:T(8,128)S(1)} %collective-permute-done.5.refs_3_) | copy-start | bytes 98308
  24.1 0.6 %copy-start.6 = (f32[64,128]{1,0:T(8,128)}, f32[64,128]{1,0:T(8,128)S(1)}, u32[]{:S(2)}) copy-start(f32[64,128]{1,0:T(8,128)S(1)} %collective-permute-done.4.refs_2_) | copy-start | bytes 98308
  24.1 0.6 %copy-start.9 = (f32[64,128]{1,0:T(8,128)}, f32[64,128]{1,0:T(8,128)S(1)}, u32[]{:S(2)}) copy-start(f32[64,128]{1,0:T(8,128)S(1)} %collective-permute-done.3.refs_1_) | copy-start | bytes 98308
  29.4 3.6 %collective-permute-start.8 = (f32[64,128]{1,0:T(8,128)}, f32[64,128]{1,0:T(8,128)S(1)}, u32[]{:S(2)}, u32[]{:S(2)}) collective-permute-start(f32[64,128]{1,0:T(8,128)} %get-tuple-element.26.refs_0_), channel_id=1, source_target_pairs={{0,3},{1,2},{2,1},{3,0},{4,7},{5,6},{6,5},{7,4},{8,11},{9,10},{10,... | collective-permute-start | bytes 98312 | tf_op jit(solution)/shard_map/ppermute | solution.py:331
  29.7 4.2 %collective-permute-start.7 = (f32[64,128]{1,0:T(8,128)}, f32[64,128]{1,0:T(8,128)S(1)}, u32[]{:S(2)}, u32[]{:S(2)}) collective-permute-start(f32[64,128]{1,0:T(8,128)} %get-tuple-element.26.refs_0_), channel_id=1, source_target_pairs={{0,2},{1,3},{2,0},{3,1},{4,6},{5,7},{6,4},{7,5},{8,10},{9,11},{10,... | collective-permute-start | bytes 98312 | tf_op jit(solution)/shard_map/ppermute | solution.py:331
  30.3 3.5 %collective-permute-start.6 = (f32[64,128]{1,0:T(8,128)}, f32[64,128]{1,0:T(8,128)S(1)}, u32[]{:S(2)}, u32[]{:S(2)}) collective-permute-start(f32[64,128]{1,0:T(8,128)} %get-tuple-element.26.refs_0_), channel_id=1, source_target_pairs={{0,1},{1,0},{2,3},{3,2},{4,5},{5,4},{6,7},{7,6},{8,9},{9,8},{10,11... | collective-permute-start | bytes 98312 | tf_op jit(solution)/shard_map/ppermute | solution.py:331
  33.0 0.9 %copy-start.1 = (f32[64,128]{1,0:T(8,128)}, f32[64,128]{1,0:T(8,128)S(1)}, u32[]{:S(2)}) copy-start(f32[64,128]{1,0:T(8,128)S(1)} %collective-permute-done.8.refs_3_) | copy-start | bytes 98308
  33.9 0.6 %copy-start.4 = (f32[64,128]{1,0:T(8,128)}, f32[64,128]{1,0:T(8,128)S(1)}, u32[]{:S(2)}) copy-start(f32[64,128]{1,0:T(8,128)S(1)} %collective-permute-done.7.refs_2_) | copy-start | bytes 98308
  33.9 0.6 %copy-start.7 = (f32[64,128]{1,0:T(8,128)}, f32[64,128]{1,0:T(8,128)S(1)}, u32[]{:S(2)}) copy-start(f32[64,128]{1,0:T(8,128)S(1)} %collective-permute-done.6.refs_1_) | copy-start | bytes 98308
  39.2 4.0 %collective-permute-start.11 = (f32[64,128]{1,0:T(8,128)}, f32[64,128]{1,0:T(8,128)S(1)}, u32[]{:S(2)}, u32[]{:S(2)}) collective-permute-start(f32[64,128]{1,0:T(8,128)} %get-tuple-element.28.refs_0_), channel_id=1, source_target_pairs={{0,3},{1,2},{2,1},{3,0},{4,7},{5,6},{6,5},{7,4},{8,11},{9,10},{10,... | collective-permute-start | bytes 98312 | tf_op jit(solution)/shard_map/ppermute | solution.py:331
  39.7 4.1 %collective-permute-start.10 = (f32[64,128]{1,0:T(8,128)}, f32[64,128]{1,0:T(8,128)S(1)}, u32[]{:S(2)}, u32[]{:S(2)}) collective-permute-start(f32[64,128]{1,0:T(8,128)} %get-tuple-element.28.refs_0_), channel_id=1, source_target_pairs={{0,2},{1,3},{2,0},{3,1},{4,6},{5,7},{6,4},{7,5},{8,10},{9,11},{10,... | collective-permute-start | bytes 98312 | tf_op jit(solution)/shard_map/ppermute | solution.py:331
  40.7 3.2 %collective-permute-start.9 = (f32[64,128]{1,0:T(8,128)}, f32[64,128]{1,0:T(8,128)S(1)}, u32[]{:S(2)}, u32[]{:S(2)}) collective-permute-start(f32[64,128]{1,0:T(8,128)} %get-tuple-element.28.refs_0_), channel_id=1, source_target_pairs={{0,1},{1,0},{2,3},{3,2},{4,5},{5,4},{6,7},{7,6},{8,9},{9,8},{10,11... | collective-permute-start | bytes 98312 | tf_op jit(solution)/shard_map/ppermute | solution.py:331
  43.1 0.7 %copy-start.10 = (f32[64,128]{1,0:T(8,128)}, f32[64,128]{1,0:T(8,128)S(1)}, u32[]{:S(2)}) copy-start(f32[64,128]{1,0:T(8,128)S(1)} %collective-permute-done.11.refs_3_) | copy-start | bytes 98308
  43.9 0.6 %copy-start.11 = (f32[64,128]{1,0:T(8,128)}, f32[64,128]{1,0:T(8,128)S(1)}, u32[]{:S(2)}) copy-start(f32[64,128]{1,0:T(8,128)S(1)} %collective-permute-done.10.refs_2_) | copy-start | bytes 98308
  43.9 0.6 %copy-start.12 = (f32[64,128]{1,0:T(8,128)}, f32[64,128]{1,0:T(8,128)S(1)}, u32[]{:S(2)}) copy-start(f32[64,128]{1,0:T(8,128)S(1)} %collective-permute-done.9.refs_1_) | copy-start | bytes 98308
  46.3 5.0 %collective-permute-start.14 = (f32[40,128]{1,0:T(8,128)}, f32[40,128]{1,0:T(8,128)S(1)}, u32[]{:S(2)}, u32[]{:S(2)}) collective-permute-start(f32[40,128]{1,0:T(8,128)} %get-tuple-element.31), channel_id=1, source_target_pairs={{0,12},{4,8},{8,4},{12,0},{16,28},{20,24},{24,20},{28,16},{1,13},{... | collective-permute-start | bytes 61448 | tf_op jit(solution)/shard_map/ppermute | solution.py:331
  48.8 4.0 %collective-permute-start.13 = (f32[40,128]{1,0:T(8,128)}, f32[40,128]{1,0:T(8,128)S(1)}, u32[]{:S(2)}, u32[]{:S(2)}) collective-permute-start(f32[40,128]{1,0:T(8,128)} %get-tuple-element.31), channel_id=1, source_target_pairs={{0,8},{4,12},{8,0},{12,4},{16,24},{20,28},{24,16},{28,20},{1,9},{5... | collective-permute-start | bytes 61448 | tf_op jit(solution)/shard_map/ppermute | solution.py:331
  49.2 4.0 %collective-permute-start.12 = (f32[40,128]{1,0:T(8,128)}, f32[40,128]{1,0:T(8,128)S(1)}, u32[]{:S(2)}, u32[]{:S(2)}) collective-permute-start(f32[40,128]{1,0:T(8,128)} %get-tuple-element.31), channel_id=1, source_target_pairs={{0,4},{4,0},{8,12},{12,8},{16,20},{20,16},{24,28},{28,24},{1,5},{5... | collective-permute-start | bytes 61448 | tf_op jit(solution)/shard_map/ppermute | solution.py:331
  54.0 4.7 %copy-start = (f32[40,128]{1,0:T(8,128)}, f32[40,128]{1,0:T(8,128)S(1)}, u32[]{:S(2)}) copy-start(f32[40,128]{1,0:T(8,128)S(1)} %add_add_fusion.refs_0_) | copy-start | bytes 61444
  54.0 4.7 %collective-permute-start.15 = (f32[40,128]{1,0:T(8,128)S(1)}, f32[40,128]{1,0:T(8,128)S(1)}, u32[]{:S(2)}, u32[]{:S(2)}) collective-permute-start(f32[40,128]{1,0:T(8,128)S(1)} %add_add_fusion.refs_0_), channel_id=1, source_target_pairs={{0,16},{4,20},{8,24},{12,28},{16,0},{20,4},{24,8},{28,12},{1,17},{... | collective-permute-start | bytes 61448 | tf_op jit(solution)/shard_map/ppermute | solution.py:331
  58.7 0.6 copy-start.13
